TPU v7x, 32 devices: a whole 2x2x4 slice. The times are simulated.
32 devices in a mesh: rep: 2 (over x), dp: 16 (over y, z, core).
Axes of the slice: x: 2, y: 2, z: 4, core: 2. Of those that a mesh axis runs over, the one named last changes fastest.
Arguments:
- x: bfloat16 [32, 2048, 1024], P(('rep', 'dp')), parts along dimension 0
- dy: bfloat16 [32, 2048, 1024], P(('rep', 'dp')), parts along dimension 0
- w_gate: bfloat16 [2, 1024, 2816], replicated
- w_up: bfloat16 [2, 1024, 2816], replicated
- w_down: bfloat16 [2, 2816, 1024], replicated
- m_w_gate: float32 [2, 1024, 2816], P(None, 'dp')
- m_w_up: float32 [2, 1024, 2816], P(None, 'dp')
- m_w_down: float32 [2, 2816, 1024], P(None, 'dp')
- v_w_gate: float32 [2, 1024, 2816], P(None, 'dp')
- v_w_up: float32 [2, 1024, 2816], P(None, 'dp')
- v_w_down: float32 [2, 2816, 1024], P(None, 'dp')
Outputs:
- output 1: bfloat16 [4, 1024, 2816], P('rep'), parts along dimension 0
- output 2: bfloat16 [4, 1024, 2816], P('rep'), parts along dimension 0
- output 3: bfloat16 [4, 2816, 1024], P('rep'), parts along dimension 0
- output 4: float32 [4, 1024, 2816], P('rep', 'dp'), parts along dimension 0
- output 5: float32 [4, 1024, 2816], P('rep', 'dp'), parts along dimension 0
- output 6: float32 [4, 2816, 1024], P('rep', 'dp'), parts along dimension 0
- output 7: float32 [4, 1024, 2816], P('rep', 'dp'), parts along dimension 0
- output 8: float32 [4, 1024, 2816], P('rep', 'dp'), parts along dimension 0
- output 9: float32 [4, 2816, 1024], P('rep', 'dp'), parts along dimension 0
There are 2 independent parts. A program takes and returns all parts, laid end to end along the dimension named above; an argument that names none is the same for every part.
All inputs are finite; a program needn't handle non-finite values.
Results may differ from a plain program's by a relative error of at most 0.02.
Values are sent between devices in bfloat16 or wider.
A program may use at most 2 GiB of HBM per device.

v0:
```python
import jax
import jax.numpy as jnp
from jax import lax

NAMES = ("w_gate", "w_up", "w_down")


def matmul(a, w):
    return jnp.dot(a, w, preferred_element_type=jnp.float32).astype(jnp.bfloat16)


def normed(h):
    wide = h.astype(jnp.float32)
    scale = lax.rsqrt(jnp.mean(wide**2, -1, keepdims=True) + 1e-6)
    return (wide * scale).astype(jnp.bfloat16)


def layer(h, w):
    a = normed(h)
    gate = jnp.dot(a, w["w_gate"], preferred_element_type=jnp.float32)
    up = jnp.dot(a, w["w_up"], preferred_element_type=jnp.float32)
    return h + matmul((jax.nn.silu(gate) * up).astype(jnp.bfloat16), w["w_down"])


def adamw(w, m, v, g):
    m = 0.9 * m + 0.1 * g
    v = 0.95 * v + 0.05 * g * g
    step = m * lax.rsqrt(v + 1e-8) + 0.1 * w
    return (w - 0.02 * step).astype(jnp.bfloat16), m, v


def stack(weights, h):
    for number in range(weights["w_gate"].shape[0]):
        h = layer(h, {name: w[number] for name, w in weights.items()})
    return h


def solution(mesh):
    groups = mesh.shape["rep"]

    def step(x, dy, *arrays):
        weights, m, v = (arrays[i : i + 3] for i in (0, 3, 6))
        x, dy = (t.reshape(groups, -1, *t.shape[1:]) for t in (x, dy))

        def of_a_group(x, dy):
            _, back = jax.vjp(lambda w: stack(w, x), dict(zip(NAMES, weights, strict=True)))
            by_weights = back(dy)[0]
            gradients = [by_weights[name].astype(jnp.float32) for name in NAMES]
            new = [adamw(w.astype(jnp.float32), m, v, g) for w, m, v, g in zip(weights, m, v, gradients, strict=True)]
            return tuple(one[which] for which in range(3) for one in new)

        return tuple(t.reshape(-1, *t.shape[2:]) for t in jax.vmap(of_a_group)(x, dy))

    return step
```

profile of v0, /device:TPU:0, one launch (start us, length us, event | category | flops | bytes accessed | tf_op | source)
XLA Modules:
  0.0 1610.3 jit_solution(11562708194355261995)
XLA Ops:
  22.5 18.2 %fusion.180 = f32[2048,2816]{1,0:T(8,128)} fusion(bf16[2,1024,2816]{2,1,0:T(8,128)(2,1)} %param.12, bf16[1,2048,1024]{2,1,0:T(8,128)(2,1)S(1)} %copy-done.6, f32[2048]{0:T(1024)S(1)} %add_rsqrt_fusion), kind=kOutput, calls=%fused_computation.228 | convolution fusion | flops 11817451520 | bytes 33038336 | tf_op jit(solution)/vmap(jvp())/dot_general | solution.py:20
  40.6 28.6 %fusion.156 = (bf16[1,1,2048,2816]{3,2,1,0:T(8,128)(2,1)}, f32[2048,2816]{1,0:T(8,128)}) fusion(f32[2048,2816]{1,0:T(8,128)} %fusion.180, bf16[2,1024,2816]{2,1,0:T(8,128)(2,1)} %param.15, bf16[1,2048,1024]{2,1,0:T(8,128)(2,1)} %param.14, f32[2048]{0:T(1024)S(1)} %add_rsqrt_fusion), kind=kOutput, calls=%fused_computation.191 | convolution fusion | flops 11852054528 | bytes 67641344 | tf_op jit(solution)/vmap(jvp())/dot_general | solution.py:21
  69.3 19.5 %fusion.166 = (f32[2048]{0:T(1024)S(1)}, bf16[1,1,2048,1024]{2,3,1,0:T(8,128)(2,1)}) fusion(bf16[2,2816,1024]{2,1,0:T(8,128)(2,1)} %param.16, bf16[1,1,2048,2816]{3,2,1,0:T(8,128)(2,1)} %get-tuple-element.263, bf16[1,2048,1024]{1,2,0:T(8,128)(2,1)} %copy), kind=kOutput, calls=%fused_computation.213 | convolution fusion | flops 11821643776 | bytes 25698304 | tf_op jit(solution)/vmap(jvp())/dot_general | solution.py:9
  92.7 19.6 %fusion.169 = f32[2048,2816]{1,0:T(8,128)} fusion(bf16[2,1024,2816]{2,1,0:T(8,128)(2,1)} %param.12, bf16[1,1,2048,1024]{2,3,1,0:T(8,128)(2,1)S(1)} %fusion.167), kind=kOutput, calls=%fused_computation.217 | convolution fusion | flops 11811160064 | bytes 33030144 | tf_op jit(solution)/vmap(jvp())/dot_general | solution.py:20
  112.3 26.8 %fusion.155 = (bf16[1,1,2048,2816]{3,2,1,0:T(8,128)(2,1)}, f32[2048,2816]{1,0:T(8,128)}) fusion(f32[2048,2816]{1,0:T(8,128)} %fusion.169, bf16[2,1024,2816]{2,1,0:T(8,128)(2,1)} %param.15, bf16[1,1,2048,1024]{2,3,1,0:T(8,128)(2,1)S(1)} %fusion.167), kind=kOutput, calls=%fused_computation.189 | convolution fusion | flops 11845763072 | bytes 67633152 | tf_op jit(solution)/vmap(jvp())/dot_general | solution.py:21
  145.7 33.6 %convert_multiply_fusion.2 = (bf16[1,1,2048,2816]{3,2,1,0:T(8,128)(2,1)}, bf16[1,1,2048,2816]{3,2,1,0:T(8,128)(2,1)}) fusion(f32[2048,2816]{1,0:T(8,128)} %fusion.169, f32[2048,2816]{1,0:T(8,128)} %get-tuple-element.270, bf16[2,2816,1024]{2,1,0:T(8,128)(2,1)} %param.16, bf16[1,2048,1024]{2,1,0:T(8,128)(2,1)} %param.17), kind=kOutput, calls=%fused_computation.172 | convolution fusion | flops 11903434752 | bytes 79167488 | tf_op jit(solution)/vmap(transpose(jvp()))/dot_general | solution.py:9
  179.3 18.1 %fusion.148 = bf16[2048,1024]{0,1:T(8,128)(2,1)} fusion(bf16[1,1,2048,2816]{3,2,1,0:T(8,128)(2,1)} %get-tuple-element.545, bf16[2,1024,2816]{2,1,0:T(8,128)(2,1)} %param.12), kind=kOutput, calls=%fused_computation.178 | convolution fusion | flops 11811160064 | bytes 21495808 | tf_op jit(solution)/vmap(transpose(jvp()))/dot_general | solution.py:20
  197.4 19.4 %fusion.168 = (f32[2048]{0:T(1024)S(1)}, bf16[2048,1024]{0,1:T(8,128)(2,1)}) fusion(bf16[1,1,2048,1024]{2,3,1,0:T(8,128)(2,1)S(1)} %copy-done.5, bf16[2048,1024]{0,1:T(8,128)(2,1)} %fusion.148, bf16[2,1024,2816]{2,1,0:T(8,128)(2,1)} %param.15, bf16[1,1,2048,2816]{3,2,1,0:T(8,128)(2,1)} %get-tuple-element.623), kind=kOutput, calls=%fused_computation.215 | convolution fusion | flops 11821643776 | bytes 29892608 | tf_op jit(solution)/vmap(transpose(jvp()))/dot_general | solution.py:21
  216.9 7.6 fusion.191
  224.5 33.8 %convert_multiply_fusion = (bf16[1,1,2048,2816]{3,2,1,0:T(8,128)(2,1)}, bf16[1,1,2048,2816]{3,2,1,0:T(8,128)(2,1)}) fusion(f32[2048,2816]{1,0:T(8,128)} %fusion.180, f32[2048,2816]{1,0:T(8,128)} %get-tuple-element.264, bf16[2,2816,1024]{2,1,0:T(8,128)(2,1)} %param.16, bf16[1,1,2048,1024]{2,3,1,0:T(8,128)(2,1)} %fusion.191), kind=kOutput, calls=%fused_computation.170 | convolution fusion | flops 11903434752 | bytes 79167488 | tf_op jit(solution)/vmap(transpose(jvp()))/dot_general | solution.py:9
  258.3 168.1 %while.13 = (bf16[1,1,2048,1024]{2,3,1,0:T(8,128)(2,1)}, bf16[1,1,2048,2816]{3,2,1,0:T(8,128)(2,1)}, f32[1,64,2816]{2,1,0:T(8,128)}, f32[1,64,2816]{2,1,0:T(8,12...) while((bf16[1,1,2048,1024]{2,3,1,0:T(8,128)(2,1)}, ...), condition=%wide.windowed_dot_general_cond_rs.1.clone, body=%wide.windowed_dot_general_body_rs.1.clone.sunk | while | flops 2955968512 | bytes 108790480 | solution.py:20
  286.4 11.9 collective-permute-done.6
  327.8 11.3 collective-permute-done.6
  367.9 12.8 collective-permute-done.6
  411.3 13.9 collective-permute-done.6
  426.5 183.7 %while.12 = (bf16[1,1,2048,1024]{2,3,1,0:T(8,128)(2,1)}, bf16[1,1,2048,2816]{3,2,1,0:T(8,128)(2,1)}, f32[1,64,2816]{2,1,0:T(8,128)}, f32[1,64,2816]{2,1,0:T(8,12...) while((bf16[1,1,2048,1024]{2,3,1,0:T(8,128)(2,1)}, ...), condition=%wide.windowed_dot_general_cond_rs.clone, body=%wide.windowed_dot_general_body_rs.clone.sunk | while | flops 2955968512 | bytes 108790480 | solution.py:20
  441.6 13.8 collective-permute-done
  463.0 13.1 collective-permute-done.2
  505.8 14.3 collective-permute-done.2
  551.4 11.4 collective-permute-done.2
  594.3 14.6 collective-permute-done.2
  610.2 186.4 %while.15 = (bf16[1,1,2048,1024]{2,3,1,0:T(8,128)(2,1)}, bf16[1,1,2048,2816]{3,2,1,0:T(8,128)(2,1)}, f32[1,64,2816]{2,1,0:T(8,128)}, f32[1,64,2816]{2,1,0:T(8,12...) while((bf16[1,1,2048,1024]{2,3,1,0:T(8,128)(2,1)}, ...), condition=%wide.windowed_dot_general_cond_rs.3.clone, body=%wide.windowed_dot_general_body_rs.3.clone.sunk | while | flops 2955968512 | bytes 108790480 | solution.py:21
  625.5 13.6 collective-permute-done.12
  646.7 10.5 collective-permute-done.14
  689.0 12.2 collective-permute-done.14
  726.2 9.0 collective-permute-start.14
  780.8 14.6 collective-permute-done.14
  804.8 234.4 %while.14 = (bf16[1,1,2048,1024]{2,3,1,0:T(8,128)(2,1)}, bf16[1,1,2048,2816]{3,2,1,0:T(8,128)(2,1)}, f32[1,64,2816]{2,1,0:T(8,128)}, f32[1,64,2816]{2,1,0:T(8,12...) while((bf16[1,1,2048,1024]{2,3,1,0:T(8,128)(2,1)}, ...), condition=%wide.windowed_dot_general_cond_rs.2.clone, body=%wide.windowed_dot_general_body_rs.2.clone.sunk | while | flops 2955968512 | bytes 108790480 | solution.py:21
  829.5 21.0 %collective-permute-start.10 = (f32[1,64,2816]{2,1,0:T(8,128)S(1)}, f32[1,64,2816]{2,1,0:T(8,128)S(1)}, u32[]{:S(2)}, u32[]{:S(2)}) collective-permute-start(f32[1,64,2816]{2,1,0:T(8,128)S(1)} %get-tuple-element.474), channel_id=18, source_target_pairs={{0,1},{1,2},{2,3},{3,4},{4,5},{5,6},{6,7},{7,8},{8,9},{9,10},{10,1... | collective-permute-start | bytes 2162696 | tf_op jit(solution)/vmap(transpose(jvp()))/dot_general | solution.py:21
  852.2 13.3 collective-permute-done.10
  886.8 18.6 %collective-permute-done.8 = f32[1,64,2816]{2,1,0:T(8,128)} collective-permute-done((f32[1,64,2816]{2,1,0:T(8,128)}, f32[1,64,2816]{2,1,0:T(8,128)}, u32[]{:S(2)}, u32[]{:S(2)}) %collective-permute-start.8) | collective-permute-done | bytes 720928 | tf_op jit(solution)/vmap(transpose(jvp()))/dot_general | solution.py:21
  910.5 23.5 %collective-permute-start.10 = (f32[1,64,2816]{2,1,0:T(8,128)S(1)}, f32[1,64,2816]{2,1,0:T(8,128)S(1)}, u32[]{:S(2)}, u32[]{:S(2)}) collective-permute-start(f32[1,64,2816]{2,1,0:T(8,128)S(1)} %get-tuple-element.474), channel_id=18, source_target_pairs={{0,1},{1,2},{2,3},{3,4},{4,5},{5,6},{6,7},{7,8},{8,9},{9,10},{10,1... | collective-permute-start | bytes 2162696 | tf_op jit(solution)/vmap(transpose(jvp()))/dot_general | solution.py:21
  935.8 8.1 collective-permute-done.10
  979.6 14.9 collective-permute-done.10
  1026.2 11.8 collective-permute-done.10
  1040.8 11.8 collective-permute-done.26
  1057.6 15.5 copy.4
  1079.5 199.5 %while.17 = (bf16[1,1,2048,2816]{2,3,1,0:T(8,128)(2,1)}, bf16[1,1,2048,1024]{3,2,1,0:T(8,128)(2,1)}, f32[1,176,1024]{2,1,0:T(8,128)S(1)}, f32[1,176,1024]{2,1,0:...) while((bf16[1,1,2048,2816]{2,3,1,0:T(8,128)(2,1)}, ...), condition=%wide.windowed_dot_general_cond_rs.5.clone, body=%wide.windowed_dot_general_body_rs.5.clone.sunk | while | flops 2959638528 | bytes 57410148 | solution.py:9
  1091.3 15.6 collective-permute-done.20
  1116.6 26.1 %collective-permute-done.22 = f32[1,176,1024]{2,1,0:T(8,128)S(1)} collective-permute-done((f32[1,176,1024]{2,1,0:T(8,128)S(1)}, f32[1,176,1024]{2,1,0:T(8,128)S(1)}, u32[]{:S(2)}, u32[]{:S(2)}) %collective-permute-start.22) | collective-permute-done | bytes 720928 | tf_op jit(solution)/vmap(transpose(jvp()))/dot_general | solution.py:9
  1156.7 23.0 %collective-permute-done.20 = f32[1,176,1024]{2,1,0:T(8,128)S(1)} collective-permute-done((f32[1,176,1024]{2,1,0:T(8,128)S(1)}, f32[1,176,1024]{2,1,0:T(8,128)S(1)}, u32[]{:S(2)}, u32[]{:S(2)}) %collective-permute-start.20) | collective-permute-done | bytes 720928 | tf_op jit(solution)/vmap(transpose(jvp()))/dot_general | solution.py:9
  1189.4 11.0 collective-permute-done.22
  1281.1 15.2 copy.2
  1302.8 163.5 %while.16 = (bf16[1,1,2048,2816]{2,3,1,0:T(8,128)(2,1)}, bf16[1,1,2048,1024]{3,2,1,0:T(8,128)(2,1)}, f32[1,176,1024]{2,1,0:T(8,128)S(1)}, f32[1,176,1024]{2,1,0:...) while((bf16[1,1,2048,2816]{2,3,1,0:T(8,128)(2,1)}, ...), condition=%wide.windowed_dot_general_cond_rs.4.clone, body=%wide.windowed_dot_general_body_rs.4.clone.sunk | while | flops 2959638528 | bytes 57410148 | solution.py:9
  1332.0 8.0 collective-permute-done.18
  1469.4 10.4 collective-permute-done.28
  1483.8 95.6 %all-gather.14.cloned.1.call-done = bf16[1,2,2816,1024]{3,2,1,0:T(8,128)(2,1)} async-done(((bf16[1,2,176,1024]{3,2,1,0:T(8,128)(2,1)}), bf16[1,2,2816,1024]{3,2,1,0:T(8,128)(2,1)}) %all-gather.14.cloned.1.call-update) | async-done | bytes 11534352 | tf_op jit(solution)/reshape | solution.py:52
  1579.3 11.7 copy.63
  (568 shorter events, 788.3 us)
Async XLA Ops:
  7.2 1476.5 %all-gather.10.cloned.1.call-start = ((), (), s32[]{:S(2)}) async-start(), calls=%async_computation | async-start | bytes 12255232 | tf_op jit(solution)/reshape | solution.py:52
  259.4 18.7 %collective-permute-start.4 = (f32[1,64,2816]{2,1,0:T(8,128)}, f32[1,64,2816]{2,1,0:T(8,128)}, u32[]{:S(2)}, u32[]{:S(2)}) collective-permute-start(f32[1,64,2816]{2,1,0:T(8,128)} %broadcast_select_fusion.26), channel_id=9, source_target_pairs={{0,1},{1,2},{2,3},{3,4},{4,5},{5,6},{6,7},{7,8},{8,9},{9,10},{10,1... | collective-permute-start | bytes 2162696 | tf_op jit(solution)/vmap(transpose(jvp()))/dot_general | solution.py:20
  361.7 19.0 %collective-permute-start.6 = (f32[1,64,2816]{2,1,0:T(8,128)S(1)}, f32[1,64,2816]{2,1,0:T(8,128)S(1)}, u32[]{:S(2)}, u32[]{:S(2)}) collective-permute-start(f32[1,64,2816]{2,1,0:T(8,128)S(1)} %get-tuple-element.465), channel_id=11, source_target_pairs={{0,1},{1,2},{2,3},{3,4},{4,5},{5,6},{6,7},{7,8},{8,9},{9,10},{10,1... | collective-permute-start | bytes 2162696 | tf_op jit(solution)/vmap(transpose(jvp()))/dot_general | solution.py:20
  361.8 18.9 %collective-permute-start.7 = (f32[1,64,2816]{2,1,0:T(8,128)S(1)}, f32[1,64,2816]{2,1,0:T(8,128)S(1)}, u32[]{:S(2)}, u32[]{:S(2)}) collective-permute-start(f32[1,64,2816]{2,1,0:T(8,128)S(1)} %get-tuple-element.466), channel_id=10, source_target_pairs={{0,15},{1,0},{2,1},{3,2},{4,3},{5,4},{6,5},{7,6},{8,7},{9,8},{10,9... | collective-permute-start | bytes 2162696 | tf_op jit(solution)/vmap(transpose(jvp()))/dot_general | solution.py:20
  384.1 19.6 %collective-permute-start.4 = (f32[1,64,2816]{2,1,0:T(8,128)}, f32[1,64,2816]{2,1,0:T(8,128)}, u32[]{:S(2)}, u32[]{:S(2)}) collective-permute-start(f32[1,64,2816]{2,1,0:T(8,128)} %broadcast_select_fusion.26), channel_id=9, source_target_pairs={{0,1},{1,2},{2,3},{3,4},{4,5},{5,6},{6,7},{7,8},{8,9},{9,10},{10,1... | collective-permute-start | bytes 2162696 | tf_op jit(solution)/vmap(transpose(jvp()))/dot_general | solution.py:20
  405.1 20.1 %collective-permute-start.6 = (f32[1,64,2816]{2,1,0:T(8,128)S(1)}, f32[1,64,2816]{2,1,0:T(8,128)S(1)}, u32[]{:S(2)}, u32[]{:S(2)}) collective-permute-start(f32[1,64,2816]{2,1,0:T(8,128)S(1)} %get-tuple-element.465), channel_id=11, source_target_pairs={{0,1},{1,2},{2,3},{3,4},{4,5},{5,6},{6,7},{7,8},{8,9},{9,10},{10,1... | collective-permute-start | bytes 2162696 | tf_op jit(solution)/vmap(transpose(jvp()))/dot_general | solution.py:20
  405.2 20.0 %collective-permute-start.7 = (f32[1,64,2816]{2,1,0:T(8,128)S(1)}, f32[1,64,2816]{2,1,0:T(8,128)S(1)}, u32[]{:S(2)}, u32[]{:S(2)}) collective-permute-start(f32[1,64,2816]{2,1,0:T(8,128)S(1)} %get-tuple-element.466), channel_id=10, source_target_pairs={{0,15},{1,0},{2,1},{3,2},{4,3},{5,4},{6,5},{7,6},{8,7},{9,8},{10,9... | collective-permute-start | bytes 2162696 | tf_op jit(solution)/vmap(transpose(jvp()))/dot_general | solution.py:20
  426.5 371.7 %collective-permute-start.25 = (f32[1,64,2816]{2,1,0:T(8,128)}, f32[1,64,2816]{2,1,0:T(8,128)}, u32[]{:S(2)}, u32[]{:S(2)}) collective-permute-start(f32[1,64,2816]{2,1,0:T(8,128)} %get-tuple-element.39), channel_id=12, source_target_pairs={{0,1},{1,2},{2,3},{3,4},{4,5},{5,6},{6,7},{7,8},{8,9},{9,10},{10,1... | collective-permute-start | bytes 2162696 | tf_op jit(solution)/vmap(transpose(jvp()))/dot_general | solution.py:20
  427.4 27.9 %collective-permute-start = (f32[1,64,2816]{2,1,0:T(8,128)}, f32[1,64,2816]{2,1,0:T(8,128)}, u32[]{:S(2)}, u32[]{:S(2)}) collective-permute-start(f32[1,64,2816]{2,1,0:T(8,128)} %broadcast_select_fusion.24), channel_id=3, source_target_pairs={{0,1},{1,2},{2,3},{3,4},{4,5},{5,6},{6,7},{7,8},{8,9},{9,10},{10,1... | collective-permute-start | bytes 2162696 | tf_op jit(solution)/vmap(transpose(jvp()))/dot_general | solution.py:20
  428.3 27.0 %collective-permute-start.1 = (f32[1,64,2816]{2,1,0:T(8,128)}, f32[1,64,2816]{2,1,0:T(8,128)}, u32[]{:S(2)}, u32[]{:S(2)}) collective-permute-start(f32[1,64,2816]{2,1,0:T(8,128)} %broadcast_select_fusion.25), channel_id=2, source_target_pairs={{0,15},{1,0},{2,1},{3,2},{4,3},{5,4},{6,5},{7,6},{8,7},{9,8},{10,9... | collective-permute-start | bytes 2162696 | tf_op jit(solution)/vmap(transpose(jvp()))/dot_general | solution.py:20
  456.8 19.3 %collective-permute-start.2 = (f32[1,64,2816]{2,1,0:T(8,128)S(1)}, f32[1,64,2816]{2,1,0:T(8,128)S(1)}, u32[]{:S(2)}, u32[]{:S(2)}) collective-permute-start(f32[1,64,2816]{2,1,0:T(8,128)S(1)} %get-tuple-element.456), channel_id=5, source_target_pairs={{0,1},{1,2},{2,3},{3,4},{4,5},{5,6},{6,7},{7,8},{8,9},{9,10},{10,1... | collective-permute-start | bytes 2162696 | tf_op jit(solution)/vmap(transpose(jvp()))/dot_general | solution.py:20
  456.9 19.2 %collective-permute-start.3 = (f32[1,64,2816]{2,1,0:T(8,128)S(1)}, f32[1,64,2816]{2,1,0:T(8,128)S(1)}, u32[]{:S(2)}, u32[]{:S(2)}) collective-permute-start(f32[1,64,2816]{2,1,0:T(8,128)S(1)} %get-tuple-element.457), channel_id=4, source_target_pairs={{0,15},{1,0},{2,1},{3,2},{4,3},{5,4},{6,5},{7,6},{8,7},{9,8},{10,9... | collective-permute-start | bytes 2162696 | tf_op jit(solution)/vmap(transpose(jvp()))/dot_general | solution.py:20
  479.5 18.6 %collective-permute-start = (f32[1,64,2816]{2,1,0:T(8,128)}, f32[1,64,2816]{2,1,0:T(8,128)}, u32[]{:S(2)}, u32[]{:S(2)}) collective-permute-start(f32[1,64,2816]{2,1,0:T(8,128)} %broadcast_select_fusion.24), channel_id=3, source_target_pairs={{0,1},{1,2},{2,3},{3,4},{4,5},{5,6},{6,7},{7,8},{8,9},{9,10},{10,1... | collective-permute-start | bytes 2162696 | tf_op jit(solution)/vmap(transpose(jvp()))/dot_general | solution.py:20
  499.7 20.5 %collective-permute-start.2 = (f32[1,64,2816]{2,1,0:T(8,128)S(1)}, f32[1,64,2816]{2,1,0:T(8,128)S(1)}, u32[]{:S(2)}, u32[]{:S(2)}) collective-permute-start(f32[1,64,2816]{2,1,0:T(8,128)S(1)} %get-tuple-element.456), channel_id=5, source_target_pairs={{0,1},{1,2},{2,3},{3,4},{4,5},{5,6},{6,7},{7,8},{8,9},{9,10},{10,1... | collective-permute-start | bytes 2162696 | tf_op jit(solution)/vmap(transpose(jvp()))/dot_general | solution.py:20
  499.7 20.4 %collective-permute-start.3 = (f32[1,64,2816]{2,1,0:T(8,128)S(1)}, f32[1,64,2816]{2,1,0:T(8,128)S(1)}, u32[]{:S(2)}, u32[]{:S(2)}) collective-permute-start(f32[1,64,2816]{2,1,0:T(8,128)S(1)} %get-tuple-element.457), channel_id=4, source_target_pairs={{0,15},{1,0},{2,1},{3,2},{4,3},{5,4},{6,5},{7,6},{8,7},{9,8},{10,9... | collective-permute-start | bytes 2162696 | tf_op jit(solution)/vmap(transpose(jvp()))/dot_general | solution.py:20
  523.6 20.2 %collective-permute-start = (f32[1,64,2816]{2,1,0:T(8,128)}, f32[1,64,2816]{2,1,0:T(8,128)}, u32[]{:S(2)}, u32[]{:S(2)}) collective-permute-start(f32[1,64,2816]{2,1,0:T(8,128)} %broadcast_select_fusion.24), channel_id=3, source_target_pairs={{0,1},{1,2},{2,3},{3,4},{4,5},{5,6},{6,7},{7,8},{8,9},{9,10},{10,1... | collective-permute-start | bytes 2162696 | tf_op jit(solution)/vmap(transpose(jvp()))/dot_general | solution.py:20
  568.0 18.6 %collective-permute-start = (f32[1,64,2816]{2,1,0:T(8,128)}, f32[1,64,2816]{2,1,0:T(8,128)}, u32[]{:S(2)}, u32[]{:S(2)}) collective-permute-start(f32[1,64,2816]{2,1,0:T(8,128)} %broadcast_select_fusion.24), channel_id=3, source_target_pairs={{0,1},{1,2},{2,3},{3,4},{4,5},{5,6},{6,7},{7,8},{8,9},{9,10},{10,1... | collective-permute-start | bytes 2162696 | tf_op jit(solution)/vmap(transpose(jvp()))/dot_general | solution.py:20
  588.1 20.8 %collective-permute-start.2 = (f32[1,64,2816]{2,1,0:T(8,128)S(1)}, f32[1,64,2816]{2,1,0:T(8,128)S(1)}, u32[]{:S(2)}, u32[]{:S(2)}) collective-permute-start(f32[1,64,2816]{2,1,0:T(8,128)S(1)} %get-tuple-element.456), channel_id=5, source_target_pairs={{0,1},{1,2},{2,3},{3,4},{4,5},{5,6},{6,7},{7,8},{8,9},{9,10},{10,1... | collective-permute-start | bytes 2162696 | tf_op jit(solution)/vmap(transpose(jvp()))/dot_general | solution.py:20
  588.2 20.8 %collective-permute-start.3 = (f32[1,64,2816]{2,1,0:T(8,128)S(1)}, f32[1,64,2816]{2,1,0:T(8,128)S(1)}, u32[]{:S(2)}, u32[]{:S(2)}) collective-permute-start(f32[1,64,2816]{2,1,0:T(8,128)S(1)} %get-tuple-element.457), channel_id=4, source_target_pairs={{0,15},{1,0},{2,1},{3,2},{4,3},{5,4},{6,5},{7,6},{8,7},{9,8},{10,9... | collective-permute-start | bytes 2162696 | tf_op jit(solution)/vmap(transpose(jvp()))/dot_general | solution.py:20
  610.2 189.4 %collective-permute-start.24 = (f32[1,64,2816]{2,1,0:T(8,128)}, f32[1,64,2816]{2,1,0:T(8,128)}, u32[]{:S(2)}, u32[]{:S(2)}) collective-permute-start(f32[1,64,2816]{2,1,0:T(8,128)} %get-tuple-element.37), channel_id=6, source_target_pairs={{0,1},{1,2},{2,3},{3,4},{4,5},{5,6},{6,7},{7,8},{8,9},{9,10},{10,1... | collective-permute-start | bytes 2162696 | tf_op jit(solution)/vmap(transpose(jvp()))/dot_general | solution.py:20
  611.3 27.7 %collective-permute-start.12 = (f32[1,64,2816]{2,1,0:T(8,128)}, f32[1,64,2816]{2,1,0:T(8,128)}, u32[]{:S(2)}, u32[]{:S(2)}) collective-permute-start(f32[1,64,2816]{2,1,0:T(8,128)} %broadcast_select_fusion.30), channel_id=22, source_target_pairs={{0,1},{1,2},{2,3},{3,4},{4,5},{5,6},{6,7},{7,8},{8,9},{9,10},{10,1... | collective-permute-start | bytes 2162696 | tf_op jit(solution)/vmap(transpose(jvp()))/dot_general | solution.py:21
  612.2 26.8 %collective-permute-start.13 = (f32[1,64,2816]{2,1,0:T(8,128)}, f32[1,64,2816]{2,1,0:T(8,128)}, u32[]{:S(2)}, u32[]{:S(2)}) collective-permute-start(f32[1,64,2816]{2,1,0:T(8,128)} %broadcast_select_fusion.31), channel_id=21, source_target_pairs={{0,15},{1,0},{2,1},{3,2},{4,3},{5,4},{6,5},{7,6},{8,7},{9,8},{10,9... | collective-permute-start | bytes 2162696 | tf_op jit(solution)/vmap(transpose(jvp()))/dot_general | solution.py:21
  660.6 20.6 %collective-permute-start.12 = (f32[1,64,2816]{2,1,0:T(8,128)}, f32[1,64,2816]{2,1,0:T(8,128)}, u32[]{:S(2)}, u32[]{:S(2)}) collective-permute-start(f32[1,64,2816]{2,1,0:T(8,128)} %broadcast_select_fusion.30), channel_id=22, source_target_pairs={{0,1},{1,2},{2,3},{3,4},{4,5},{5,6},{6,7},{7,8},{8,9},{9,10},{10,1... | collective-permute-start | bytes 2162696 | tf_op jit(solution)/vmap(transpose(jvp()))/dot_general | solution.py:21
  662.7 18.6 %collective-permute-start.13 = (f32[1,64,2816]{2,1,0:T(8,128)}, f32[1,64,2816]{2,1,0:T(8,128)}, u32[]{:S(2)}, u32[]{:S(2)}) collective-permute-start(f32[1,64,2816]{2,1,0:T(8,128)} %broadcast_select_fusion.31), channel_id=21, source_target_pairs={{0,15},{1,0},{2,1},{3,2},{4,3},{5,4},{6,5},{7,6},{8,7},{9,8},{10,9... | collective-permute-start | bytes 2162696 | tf_op jit(solution)/vmap(transpose(jvp()))/dot_general | solution.py:21
  704.6 20.2 %collective-permute-start.12 = (f32[1,64,2816]{2,1,0:T(8,128)}, f32[1,64,2816]{2,1,0:T(8,128)}, u32[]{:S(2)}, u32[]{:S(2)}) collective-permute-start(f32[1,64,2816]{2,1,0:T(8,128)} %broadcast_select_fusion.30), channel_id=22, source_target_pairs={{0,1},{1,2},{2,3},{3,4},{4,5},{5,6},{6,7},{7,8},{8,9},{9,10},{10,1... | collective-permute-start | bytes 2162696 | tf_op jit(solution)/vmap(transpose(jvp()))/dot_general | solution.py:21
  774.6 20.8 %collective-permute-start.14 = (f32[1,64,2816]{2,1,0:T(8,128)S(1)}, f32[1,64,2816]{2,1,0:T(8,128)S(1)}, u32[]{:S(2)}, u32[]{:S(2)}) collective-permute-start(f32[1,64,2816]{2,1,0:T(8,128)S(1)} %get-tuple-element.483), channel_id=24, source_target_pairs={{0,1},{1,2},{2,3},{3,4},{4,5},{5,6},{6,7},{7,8},{8,9},{9,10},{10,1... | collective-permute-start | bytes 2162696 | tf_op jit(solution)/vmap(transpose(jvp()))/dot_general | solution.py:21
  774.6 20.8 %collective-permute-start.15 = (f32[1,64,2816]{2,1,0:T(8,128)S(1)}, f32[1,64,2816]{2,1,0:T(8,128)S(1)}, u32[]{:S(2)}, u32[]{:S(2)}) collective-permute-start(f32[1,64,2816]{2,1,0:T(8,128)S(1)} %get-tuple-element.484), channel_id=23, source_target_pairs={{0,15},{1,0},{2,1},{3,2},{4,3},{5,4},{6,5},{7,6},{8,7},{9,8},{10,9... | collective-permute-start | bytes 2162696 | tf_op jit(solution)/vmap(transpose(jvp()))/dot_general | solution.py:21
  796.6 242.6 %collective-permute-start.27 = (f32[1,64,2816]{2,1,0:T(8,128)}, f32[1,64,2816]{2,1,0:T(8,128)}, u32[]{:S(2)}, u32[]{:S(2)}) collective-permute-start(f32[1,64,2816]{2,1,0:T(8,128)} %get-tuple-element.43), channel_id=25, source_target_pairs={{0,1},{1,2},{2,3},{3,4},{4,5},{5,6},{6,7},{7,8},{8,9},{9,10},{10,1... | collective-permute-start | bytes 2162696 | tf_op jit(solution)/vmap(transpose(jvp()))/dot_general | solution.py:21
  804.7 679.0 %all-gather.12.cloned.1.call-start = ((), (), s32[]{:S(2)}) async-start(), calls=%async_computation.1 | async-start | bytes 12255232 | tf_op jit(solution)/reshape | solution.py:52
  805.7 19.8 %collective-permute-start.8 = (f32[1,64,2816]{2,1,0:T(8,128)}, f32[1,64,2816]{2,1,0:T(8,128)}, u32[]{:S(2)}, u32[]{:S(2)}) collective-permute-start(f32[1,64,2816]{2,1,0:T(8,128)} %broadcast_select_fusion.28), channel_id=16, source_target_pairs={{0,1},{1,2},{2,3},{3,4},{4,5},{5,6},{6,7},{7,8},{8,9},{9,10},{10,1... | collective-permute-start | bytes 2162696 | tf_op jit(solution)/vmap(transpose(jvp()))/dot_general | solution.py:21
  806.6 21.3 %collective-permute-start.9 = (f32[1,64,2816]{2,1,0:T(8,128)}, f32[1,64,2816]{2,1,0:T(8,128)}, u32[]{:S(2)}, u32[]{:S(2)}) collective-permute-start(f32[1,64,2816]{2,1,0:T(8,128)} %broadcast_select_fusion.29), channel_id=15, source_target_pairs={{0,15},{1,0},{2,1},{3,2},{4,3},{5,4},{6,5},{7,6},{8,7},{9,8},{10,9... | collective-permute-start | bytes 2162696 | tf_op jit(solution)/vmap(transpose(jvp()))/dot_general | solution.py:21
  829.5 36.0 %collective-permute-start.10 = (f32[1,64,2816]{2,1,0:T(8,128)S(1)}, f32[1,64,2816]{2,1,0:T(8,128)S(1)}, u32[]{:S(2)}, u32[]{:S(2)}) collective-permute-start(f32[1,64,2816]{2,1,0:T(8,128)S(1)} %get-tuple-element.474), channel_id=18, source_target_pairs={{0,1},{1,2},{2,3},{3,4},{4,5},{5,6},{6,7},{7,8},{8,9},{9,10},{10,1... | collective-permute-start | bytes 2162696 | tf_op jit(solution)/vmap(transpose(jvp()))/dot_general | solution.py:21
  870.1 35.4 %collective-permute-start.8 = (f32[1,64,2816]{2,1,0:T(8,128)}, f32[1,64,2816]{2,1,0:T(8,128)}, u32[]{:S(2)}, u32[]{:S(2)}) collective-permute-start(f32[1,64,2816]{2,1,0:T(8,128)} %broadcast_select_fusion.28), channel_id=16, source_target_pairs={{0,1},{1,2},{2,3},{3,4},{4,5},{5,6},{6,7},{7,8},{8,9},{9,10},{10,1... | collective-permute-start | bytes 2162696 | tf_op jit(solution)/vmap(transpose(jvp()))/dot_general | solution.py:21
  878.0 31.1 %collective-permute-start.9 = (f32[1,64,2816]{2,1,0:T(8,128)}, f32[1,64,2816]{2,1,0:T(8,128)}, u32[]{:S(2)}, u32[]{:S(2)}) collective-permute-start(f32[1,64,2816]{2,1,0:T(8,128)} %broadcast_select_fusion.29), channel_id=15, source_target_pairs={{0,15},{1,0},{2,1},{3,2},{4,3},{5,4},{6,5},{7,6},{8,7},{9,8},{10,9... | collective-permute-start | bytes 2162696 | tf_op jit(solution)/vmap(transpose(jvp()))/dot_general | solution.py:21
  910.5 33.4 %collective-permute-start.10 = (f32[1,64,2816]{2,1,0:T(8,128)S(1)}, f32[1,64,2816]{2,1,0:T(8,128)S(1)}, u32[]{:S(2)}, u32[]{:S(2)}) collective-permute-start(f32[1,64,2816]{2,1,0:T(8,128)S(1)} %get-tuple-element.474), channel_id=18, source_target_pairs={{0,1},{1,2},{2,3},{3,4},{4,5},{5,6},{6,7},{7,8},{8,9},{9,10},{10,1... | collective-permute-start | bytes 2162696 | tf_op jit(solution)/vmap(transpose(jvp()))/dot_general | solution.py:21
  953.3 18.6 %collective-permute-start.8 = (f32[1,64,2816]{2,1,0:T(8,128)}, f32[1,64,2816]{2,1,0:T(8,128)}, u32[]{:S(2)}, u32[]{:S(2)}) collective-permute-start(f32[1,64,2816]{2,1,0:T(8,128)} %broadcast_select_fusion.28), channel_id=16, source_target_pairs={{0,1},{1,2},{2,3},{3,4},{4,5},{5,6},{6,7},{7,8},{8,9},{9,10},{10,1... | collective-permute-start | bytes 2162696 | tf_op jit(solution)/vmap(transpose(jvp()))/dot_general | solution.py:21
  973.4 21.1 %collective-permute-start.10 = (f32[1,64,2816]{2,1,0:T(8,128)S(1)}, f32[1,64,2816]{2,1,0:T(8,128)S(1)}, u32[]{:S(2)}, u32[]{:S(2)}) collective-permute-start(f32[1,64,2816]{2,1,0:T(8,128)S(1)} %get-tuple-element.474), channel_id=18, source_target_pairs={{0,1},{1,2},{2,3},{3,4},{4,5},{5,6},{6,7},{7,8},{8,9},{9,10},{10,1... | collective-permute-start | bytes 2162696 | tf_op jit(solution)/vmap(transpose(jvp()))/dot_general | solution.py:21
  973.5 21.1 %collective-permute-start.11 = (f32[1,64,2816]{2,1,0:T(8,128)S(1)}, f32[1,64,2816]{2,1,0:T(8,128)S(1)}, u32[]{:S(2)}, u32[]{:S(2)}) collective-permute-start(f32[1,64,2816]{2,1,0:T(8,128)S(1)} %get-tuple-element.475), channel_id=17, source_target_pairs={{0,15},{1,0},{2,1},{3,2},{4,3},{5,4},{6,5},{7,6},{8,7},{9,8},{10,9... | collective-permute-start | bytes 2162696 | tf_op jit(solution)/vmap(transpose(jvp()))/dot_general | solution.py:21
  998.0 20.5 %collective-permute-start.8 = (f32[1,64,2816]{2,1,0:T(8,128)}, f32[1,64,2816]{2,1,0:T(8,128)}, u32[]{:S(2)}, u32[]{:S(2)}) collective-permute-start(f32[1,64,2816]{2,1,0:T(8,128)} %broadcast_select_fusion.28), channel_id=16, source_target_pairs={{0,1},{1,2},{2,3},{3,4},{4,5},{5,6},{6,7},{7,8},{8,9},{9,10},{10,1... | collective-permute-start | bytes 2162696 | tf_op jit(solution)/vmap(transpose(jvp()))/dot_general | solution.py:21
  1057.5 521.8 %all-gather.14.cloned.1.call-start = ((), (), s32[]{:S(2)}) async-start(), calls=%async_computation.2 | async-start | bytes 12255232 | tf_op jit(solution)/reshape | solution.py:52
  1079.6 27.3 %collective-permute-start.20 = (f32[1,176,1024]{2,1,0:T(8,128)S(1)}, f32[1,176,1024]{2,1,0:T(8,128)S(1)}, u32[]{:S(2)}, u32[]{:S(2)}) collective-permute-start(f32[1,176,1024]{2,1,0:T(8,128)S(1)} %broadcast_select_fusion.34), channel_id=35, source_target_pairs={{0,1},{1,2},{2,3},{3,4},{4,5},{5,6},{6,7},{7,8},{8,9},{9,10},{10,1... | collective-permute-start | bytes 2162696 | tf_op jit(solution)/vmap(transpose(jvp()))/dot_general | solution.py:9
  1080.5 26.3 %collective-permute-start.21 = (f32[1,176,1024]{2,1,0:T(8,128)}, f32[1,176,1024]{2,1,0:T(8,128)S(1)}, u32[]{:S(2)}, u32[]{:S(2)}) collective-permute-start(f32[1,176,1024]{2,1,0:T(8,128)} %broadcast_select_fusion.35), channel_id=34, source_target_pairs={{0,15},{1,0},{2,1},{3,2},{4,3},{5,4},{6,5},{7,6},{8,7},{9,8},{10,9... | collective-permute-start | bytes 2162696 | tf_op jit(solution)/vmap(transpose(jvp()))/dot_general | solution.py:9
  1107.1 35.6 %collective-permute-start.22 = (f32[1,176,1024]{2,1,0:T(8,128)S(1)}, f32[1,176,1024]{2,1,0:T(8,128)S(1)}, u32[]{:S(2)}, u32[]{:S(2)}) collective-permute-start(f32[1,176,1024]{2,1,0:T(8,128)S(1)} %get-tuple-element.501), channel_id=37, source_target_pairs={{0,1},{1,2},{2,3},{3,4},{4,5},{5,6},{6,7},{7,8},{8,9},{9,10},{10,1... | collective-permute-start | bytes 2162696 | tf_op jit(solution)/vmap(transpose(jvp()))/dot_general | solution.py:9
  1107.2 35.6 %collective-permute-start.23 = (f32[1,176,1024]{2,1,0:T(8,128)S(1)}, f32[1,176,1024]{2,1,0:T(8,128)S(1)}, u32[]{:S(2)}, u32[]{:S(2)}) collective-permute-start(f32[1,176,1024]{2,1,0:T(8,128)S(1)} %get-tuple-element.502), channel_id=36, source_target_pairs={{0,15},{1,0},{2,1},{3,2},{4,3},{5,4},{6,5},{7,6},{8,7},{9,8},{10,9... | collective-permute-start | bytes 2162696 | tf_op jit(solution)/vmap(transpose(jvp()))/dot_general | solution.py:9
  1145.0 34.7 %collective-permute-start.20 = (f32[1,176,1024]{2,1,0:T(8,128)S(1)}, f32[1,176,1024]{2,1,0:T(8,128)S(1)}, u32[]{:S(2)}, u32[]{:S(2)}) collective-permute-start(f32[1,176,1024]{2,1,0:T(8,128)S(1)} %broadcast_select_fusion.34), channel_id=35, source_target_pairs={{0,1},{1,2},{2,3},{3,4},{4,5},{5,6},{6,7},{7,8},{8,9},{9,10},{10,1... | collective-permute-start | bytes 2162696 | tf_op jit(solution)/vmap(transpose(jvp()))/dot_general | solution.py:9
  1146.0 33.8 %collective-permute-start.21 = (f32[1,176,1024]{2,1,0:T(8,128)}, f32[1,176,1024]{2,1,0:T(8,128)S(1)}, u32[]{:S(2)}, u32[]{:S(2)}) collective-permute-start(f32[1,176,1024]{2,1,0:T(8,128)} %broadcast_select_fusion.35), channel_id=34, source_target_pairs={{0,15},{1,0},{2,1},{3,2},{4,3},{5,4},{6,5},{7,6},{8,7},{9,8},{10,9... | collective-permute-start | bytes 2162696 | tf_op jit(solution)/vmap(transpose(jvp()))/dot_general | solution.py:9
  1179.9 20.5 %collective-permute-start.22 = (f32[1,176,1024]{2,1,0:T(8,128)S(1)}, f32[1,176,1024]{2,1,0:T(8,128)S(1)}, u32[]{:S(2)}, u32[]{:S(2)}) collective-permute-start(f32[1,176,1024]{2,1,0:T(8,128)S(1)} %get-tuple-element.501), channel_id=37, source_target_pairs={{0,1},{1,2},{2,3},{3,4},{4,5},{5,6},{6,7},{7,8},{8,9},{9,10},{10,1... | collective-permute-start | bytes 2162696 | tf_op jit(solution)/vmap(transpose(jvp()))/dot_general | solution.py:9
  1279.0 189.2 %collective-permute-start.29 = (f32[1,176,1024]{2,1,0:T(8,128)}, f32[1,176,1024]{2,1,0:T(8,128)}, u32[]{:S(2)}, u32[]{:S(2)}) collective-permute-start(f32[1,176,1024]{2,1,0:T(8,128)} %get-tuple-element.47), channel_id=38, source_target_pairs={{0,1},{1,2},{2,3},{3,4},{4,5},{5,6},{6,7},{7,8},{8,9},{9,10},{10,1... | collective-permute-start | bytes 2162696 | tf_op jit(solution)/vmap(transpose(jvp()))/dot_general | solution.py:9
  (139 other events, 2602.4 us)
Sparse Core Ops, SparseCore 0:
  804.9 137.2 all-gather.9
  1057.7 123.2 all-gather.11
  1483.8 95.4 all-gather.13
where the time goes:
time: 1620 us; the launch traced here: 1610 us
  waiting for transfers between devices  598 us (37%)
  matrix products  413 us (25%)
  starting transfers between devices  265 us (16%)
  other arithmetic  173 us (11%)
  local copies, waits for them, and re-layouts  96.6 us (6%)
  loops' own time  49.1 us (3%)
    dot_general x34, waiting for transfers between devices, layer(): up = jnp.dot(a, w['w_up'], preferred_element_type=jnp.float32)  184 us
    dot_general x34, waiting for transfers between devices, matmul(): jnp.dot(a, w, preferred_element_type=jnp.float32).astype(jnp.bfloat16)  175 us
    dot_general x19, matrix products, matmul(): jnp.dot(a, w, preferred_element_type=jnp.float32).astype(jnp.bfloat16)  156 us
    dot_general x34, waiting for transfers between devices, layer(): gate = jnp.dot(a, w['w_gate'], preferred_element_type=jnp.float32)  143 us
    dot_general x19, matrix products, layer(): up = jnp.dot(a, w['w_up'], preferred_element_type=jnp.float32)  138 us
    dot_general x19, matrix products, layer(): gate = jnp.dot(a, w['w_gate'], preferred_element_type=jnp.float32)  119 us
    dot_general x34, starting transfers between devices, layer(): up = jnp.dot(a, w['w_up'], preferred_element_type=jnp.float32)  113 us
    reshape x3, waiting for transfers between devices, step(): t.reshape(-1, *t.shape[2:])  95.6 us
  transfers between devices with their start and end apart: 105, of which 73 were waited for; matrix products, arithmetic and copies ran while one was open for 24% of the time, Pallas kernels for 0%

commit v1 on v0

v1 whole, which is shorter than its diff:
```python
import functools

import jax
import jax.numpy as jnp
from jax import lax
from jax.experimental import pallas as pl
from jax.experimental.pallas import tpu as pltpu
from jax.sharding import PartitionSpec as P

F32, BF16 = jnp.float32, jnp.bfloat16
KINDS = 3
CHUNK = 256


def matmul(a, w):
    return jnp.dot(a, w, preferred_element_type=F32).astype(BF16)


def matmul_t(a, w):
    return lax.dot_general(a, w, (((1,), (1,)), ((), ())), preferred_element_type=F32).astype(BF16)


def inverse_rms(h):
    wide = h.astype(F32)
    return lax.rsqrt(jnp.mean(wide**2, -1, keepdims=True) + 1e-6)


def forward(h, wg, wu):
    scale = inverse_rms(h)
    a = (h.astype(F32) * scale).astype(BF16)
    gate = jnp.dot(a, wg, preferred_element_type=F32)
    up = jnp.dot(a, wu, preferred_element_type=F32)
    act = (jax.nn.silu(gate) * up).astype(BF16)
    return a, gate, up, act


def through_product(gate, up, dact):
    dact = dact.astype(F32)
    s = jax.nn.sigmoid(gate)
    silu = gate * s
    dgate = dact * up * (s + silu * (1 - s))
    return dgate.astype(BF16), (dact * silu).astype(BF16)


def through_norm(h, da):
    wide, da = h.astype(F32), da.astype(F32)
    scale = inverse_rms(h)
    inner = jnp.sum(da * wide, -1, keepdims=True)
    return (da * scale - wide * (scale**3 * inner / h.shape[-1])).astype(BF16)


def chain(x, dy, wg, wu, wd):
    a0, gate0, up0, act0 = forward(x, wg[0], wu[0])
    h1 = x + matmul(act0, wd[0])
    a1, gate1, up1, act1 = forward(h1, wg[1], wu[1])
    dgate1, dup1 = through_product(gate1, up1, matmul_t(dy, wd[1]))
    da = matmul_t(dgate1, wg[1]) + matmul_t(dup1, wu[1])
    dh0 = dy + through_norm(h1, da)
    dgate0, dup0 = through_product(gate0, up0, matmul_t(dh0, wd[0]))
    return (a0, dgate0, dup0, act0, dh0), (a1, dgate1, dup1, act1, dy)


def tail_kernel(ny, nz, units, *refs):
    layers = 2
    acts = [refs[5 * n : 5 * n + 5] for n in range(layers)]
    refs = refs[5 * layers :]
    ws, ms, vs, nws, nms, nvs = (refs[3 * i : 3 * i + 3] for i in range(6))
    zrecv = refs[18:20]
    (g0, g1, c0, c1, y0, y1, cs0, cs1, mst0, mst1, vst0, vst1, wst0, wst1, zst0, zst1, at, ach, bt,
     c_s, c_r, y_s, y_r, z_s, z_r, agz_s, agz_r, agy_s, agy_r, agc_s, agc_r, asem, bsem, lsem, osem) = refs[20:]
    G, C, Y, CS = (g0, g1), (c0, c1), (y0, y1), (cs0, cs1)
    MST, VST, WST, ZST = (mst0, mst1), (vst0, vst1), (wst0, wst1), (zst0, zst1)

    me = lax.axis_index("dp")
    c = lax.rem(me, 2)
    z = lax.rem(lax.div(me, 2), nz)
    y = lax.div(me, 2 * nz)

    def at_(yy, zz, cc):
        return (yy * nz + zz) * 2 + cc

    def zrel(k):
        return lax.rem(z + k + nz, nz)

    core_peer = at_(y, z, 1 - c)
    y_peer = at_(1 - y, z, c)
    z_peers = [at_(y, zrel(k), c) for k in range(1, nz)]

    def remote(src, dst, ss, rs, dev):
        return pltpu.make_async_remote_copy(
            src_ref=src, dst_ref=dst, send_sem=ss, recv_sem=rs, device_id={"dp": dev}, device_id_type=pl.DeviceIdType.MESH
        )

    barrier = pltpu.get_barrier_semaphore()
    for dev in [core_peer, y_peer, *z_peers]:
        pl.semaphore_signal(barrier, inc=1, device_id={"dp": dev}, device_id_type=pl.DeviceIdType.MESH)
    pl.semaphore_wait(barrier, 2 + len(z_peers))

    info = []
    seen = [0, 0]
    for layer, kind in units:
        t = int(kind == 2)
        info.append((layer, kind, t, seen[t]))
        seen[t] += 1

    def rows_of(t):
        return G[t].shape[3], G[t].shape[4]

    def c_copy(u, h):
        layer, kind, t, i = info[u]
        return remote(CS[t], C[t].at[i, h], c_s.at[u, h], c_r.at[u, h], core_peer)

    def y_copy(u, j):
        layer, kind, t, i = info[u]
        zz = zrel(j)
        return remote(G[t].at[i, 0, zz], Y[t].at[i, zz], y_s.at[u, j], y_r.at[u, j], y_peer)

    def z_copy(u, k):
        layer, kind, t, i = info[u]
        return remote(G[t].at[i, 1, zrel(k)], zrecv[t].at[i, k - 1], z_s.at[u, k - 1], z_r.at[u, k - 1], z_peers[k - 1])

    def spot(u, d):
        layer, kind, t, i = info[u]
        rows = rows_of(t)[0]
        return nws[kind].at[layer, pl.ds(pl.multiple_of(d * rows, rows), rows), :]

    last_c = [None, None]

    def compute(u, h):
        layer, kind, t, i = info[u]
        a, dgate, dup, act, dh = acts[layer]
        lhs, rhs = ((a, dgate), (a, dup), (act, dh))[kind]
        rows, cols = rows_of(t)
        tokens = lhs.shape[0]
        half = nz * 2 * rows
        yy = y if h else 1 - y
        steps, tiles = tokens // CHUNK, cols // CHUNK

        def get_a(s):
            where = pl.ds(pl.multiple_of(s * CHUNK, CHUNK), CHUNK)
            return pltpu.make_async_copy(lhs.at[where, pl.ds(pl.multiple_of(yy * half, 128), half)], at.at[where, :half], asem.at[0])

        def get_b(n, slot):
            return pltpu.make_async_copy(rhs.at[:, pl.ds(pl.multiple_of(n * CHUNK, CHUNK), CHUNK)], bt.at[slot], bsem.at[slot])

        whole = pltpu.make_async_copy(lhs.at[:, pl.ds(pl.multiple_of(yy * half, 128), half)], at.at[:, :half], asem.at[0])
        whole.start()
        get_b(0, 0).start()

        whole.wait()
        if last_c[t] is not None:
            c_copy(*last_c[t]).wait_send()

        @pl.loop(0, tiles)
        def _(n):
            slot = lax.rem(n, 2)

            @pl.when(n + 1 < tiles)
            def _():
                get_b(n + 1, 1 - slot).start()

            get_b(n, slot).wait()
            out = lax.dot_general(at[:, :half], bt[slot], (((0,), (0,)), ((), ())), preferred_element_type=F32).astype(BF16)
            out = out.reshape(nz, 2, rows, CHUNK)
            where = pl.ds(pl.multiple_of(n * CHUNK, CHUNK), CHUNK)
            for zz in range(nz):
                first, second = out[zz, 0], out[zz, 1]
                G[t][i, h, zz, :, where] = jnp.where(c == 0, first, second)
                CS[t][zz, :, where] = jnp.where(c == 0, second, first)

        c_copy(u, h).start()
        last_c[t] = (u, h)

    def pieces(t, body):
        rows, cols = rows_of(t)
        wide = cols // 2 if cols > 2048 else cols

        @pl.loop(0, rows // 16)
        def _(r):
            for n in range(0, cols, wide):
                body(pl.ds(pl.multiple_of(r * 16, 16), 16), pl.ds(n, wide))

    def to_y(u):
        layer, kind, t, i = info[u]
        c_copy(u, 0).wait_recv()
        for j in [*range(1, nz), 0]:
            zz = zrel(j)

            def body(r, n):
                G[t][i, 0, zz, r, n] = (G[t][i, 0, zz, r, n].astype(F32) + C[t][i, 0, zz, r, n].astype(F32)).astype(BF16)

            pieces(t, body)
            y_copy(u, j).start()

    def to_z(u):
        layer, kind, t, i = info[u]
        c_copy(u, 1).wait_recv()
        for k in range(1, nz):
            zz = zrel(k)
            y_copy(u, k).wait_recv()

            def body(r, n):
                G[t][i, 1, zz, r, n] = (
                    G[t][i, 1, zz, r, n].astype(F32) + C[t][i, 1, zz, r, n].astype(F32) + Y[t][i, zz, r, n].astype(F32)
                ).astype(BF16)

            pieces(t, body)
            z_copy(u, k).start()

    pending = [None, None]

    def moments_out(u):
        layer, kind, t, i = info[u]
        return [
            pltpu.make_async_copy(MST[t], nms[kind].at[layer], osem.at[t, 0]),
            pltpu.make_async_copy(VST[t], nvs[kind].at[layer], osem.at[t, 1]),
        ]

    def own_out(u):
        layer, kind, t, i = info[u]
        return pltpu.make_async_copy(G[t].at[i, 1, z], spot(u, me), osem.at[t, 2])

    def send(u, src, d, to, j):
        if to == "z":
            return remote(src, spot(u, d), agz_s.at[u, j], agz_r.at[u, j], z_peers[j])
        if to == "y":
            return remote(src, spot(u, d), agy_s.at[u, j], agy_r.at[u, j], y_peer)
        return remote(src, spot(u, d), agc_s.at[u, j], agc_r.at[u, j], core_peer)

    def finish(u):
        layer, kind, t, i = info[u]
        rows, cols = rows_of(t)
        if pending[t] is not None:
            for copy in moments_out(pending[t]):
                copy.wait()
            own_out(pending[t]).wait()
        loads = [
            pltpu.make_async_copy(ms[kind].at[layer], MST[t], lsem.at[t, 0]),
            pltpu.make_async_copy(vs[kind].at[layer], VST[t], lsem.at[t, 1]),
            pltpu.make_async_copy(ws[kind].at[layer, pl.ds(pl.multiple_of(me * rows, rows), rows), :], WST[t], lsem.at[t, 2]),
        ]
        for copy in loads:
            copy.start()
        y_copy(u, 0).wait_recv()
        for k in range(1, nz):
            z_copy(u, k).wait_recv()
        get_z = pltpu.make_async_copy(zrecv[t].at[i], ZST[t], lsem.at[t, 3])
        get_z.start()
        for copy in [*loads, get_z]:
            copy.wait()

        def body(r, n):
            g = G[t][i, 1, z, r, n].astype(F32) + C[t][i, 1, z, r, n].astype(F32) + Y[t][i, z, r, n].astype(F32)
            for k in range(nz - 1):
                g = g + ZST[t][k, r, n].astype(F32)
            g = g.astype(BF16).astype(F32)
            w = WST[t][r, n].astype(F32)
            m = 0.9 * MST[t][r, n] + 0.1 * g
            v = 0.95 * VST[t][r, n] + 0.05 * g * g
            MST[t][r, n] = m
            VST[t][r, n] = v
            G[t][i, 1, z, r, n] = (w - 0.02 * (m * lax.rsqrt(v + 1e-8) + 0.1 * w)).astype(BF16)

        pieces(t, body)
        mine = G[t].at[i, 1, z]
        for k in range(nz - 1):
            send(u, mine, me, "z", k).start()
        send(u, mine, me, "y", 0).start()
        send(u, mine, me, "core", 0).start()
        for copy in moments_out(u):
            copy.start()
        own_out(u).start()
        pending[t] = u

    def from_z(u):
        for k in range(1, nz):
            d = at_(y, zrel(-k), c)
            send(u, spot(u, d), d, "z", k - 1).wait_recv()
            send(u, spot(u, d), d, "y", k).start()
            send(u, spot(u, d), d, "core", k).start()

    def from_y(u):
        for j in range(nz):
            d = at_(1 - y, zrel(-j), c)
            send(u, spot(u, d), d, "y", j).wait_recv()
            send(u, spot(u, d), d, "core", nz + j).start()

    n = len(units)
    done = {name: 0 for name in "yzfab"}
    stages = {"y": to_y, "z": to_z, "f": finish, "a": from_z, "b": from_y}

    def run(text):
        for s in text:
            stages[s](done[s])
            done[s] += 1

    for u in range(n):
        compute(u, 0)
        if u:
            run("y")
        compute(u, 1)
        if u == 2:
            run("z")
        if u == 3:
            run("z")
        if u == 4:
            run("fz")
    run("y" + "fza" + "fzab" + "fzab" + "fab" + "fab" + "ab" + "b")
    assert all(v == n for v in done.values()), done

    for u in range(n):
        layer, kind, t, i = info[u]
        for h in range(2):
            if last_c[t] == (u, h):
                c_copy(u, h).wait_send()
        for j in range(nz):
            y_copy(u, j).wait_send()
        for k in range(1, nz):
            z_copy(u, k).wait_send()
            send(u, G[t].at[i, 1, z], me, "z", k - 1).wait_send()
        for j in range(nz):
            send(u, G[t].at[i, 1, z], me, "y", j).wait_send()
        for j in range(2 * nz):
            send(u, G[t].at[i, 1, z], me, "core", j).wait_send()
            d = at_(y if j < nz else 1 - y, zrel(-(j % nz)), 1 - c)
            send(u, spot(u, d), d, "core", j).wait_recv()
    for t in range(2):
        for copy in moments_out(pending[t]):
            copy.wait()
        own_out(pending[t]).wait()


def tail(ny, nz, acts, ws, ms, vs):
    units = ((1, 0), (1, 1), (1, 2), (0, 0), (0, 1), (0, 2))
    rg, ff = ms[0].shape[1:]
    rd, dim = ms[2].shape[1:]
    tokens = acts[0][0].shape[0]
    shapes = ((rg, ff), (rd, dim))
    slots = (4, 2)
    n = len(units)
    any_spec = pl.BlockSpec(memory_space=pl.ANY)
    outs = (
        [jax.ShapeDtypeStruct(w.shape, BF16) for w in ws]
        + [jax.ShapeDtypeStruct(m.shape, F32) for m in (*ms, *vs)]
        + [jax.ShapeDtypeStruct((s, nz - 1, *shape), BF16) for s, shape in zip(slots, shapes)]
    )
    scratch = (
        [pltpu.VMEM((s, 2, nz, *shape), BF16) for s, shape in zip(slots, shapes)]
        + [pltpu.VMEM((s, 2, nz, *shape), BF16) for s, shape in zip(slots, shapes)]
        + [pltpu.VMEM((s, nz, *shape), BF16) for s, shape in zip(slots, shapes)]
        + [pltpu.VMEM((nz, *shape), BF16) for shape in shapes]
        + [pltpu.VMEM(shape, F32) for shape in shapes] * 2
        + [pltpu.VMEM(shape, BF16) for shape in shapes]
        + [pltpu.VMEM((nz - 1, *shape), BF16) for shape in shapes]
    )
    half = nz * 2 * max(rg, rd)
    scratch += [
        pltpu.VMEM((tokens, half), BF16),
        pltpu.VMEM((2, 16, half), BF16),
        pltpu.VMEM((2, tokens, CHUNK), BF16),
    ]
    dma = pltpu.SemaphoreType.DMA
    for count in (2, nz, nz - 1, nz - 1, nz, 2 * nz):
        scratch += [dma((n, count)), dma((n, count))]
    scratch += [dma((2,)), dma((2,)), dma((2, 4)), dma((2, 3))]
    flops = 2 * n * tokens * ff * dim
    res = pl.pallas_call(
        functools.partial(tail_kernel, ny, nz, units),
        out_shape=outs,
        in_specs=[any_spec] * (10 + 9),
        out_specs=[any_spec] * len(outs),
        scratch_shapes=scratch,
        compiler_params=pltpu.CompilerParams(collective_id=0, has_side_effects=True, vmem_limit_bytes=67043328),
        cost_estimate=pl.CostEstimate(flops=flops, bytes_accessed=200 << 20, transcendentals=0),
        name="gradients_and_step",
    )(*acts[0], *acts[1], *ws, *ms, *vs)
    return tuple(res[:9])


def solution(mesh):
    nz = 4
    ny = mesh.shape["dp"] // (2 * nz)

    def step(x, dy, *arrays):
        ws, ms, vs = (arrays[i : i + 3] for i in (0, 3, 6))
        acts = chain(x[0], dy[0], *ws)
        return tail(ny, nz, acts, ws, ms, vs)

    mom = P(None, "dp", None)
    return jax.shard_map(
        step,
        mesh=mesh,
        in_specs=(P(("rep", "dp")),) * 2 + (P(),) * 3 + (mom,) * 6,
        out_specs=(P("rep"),) * 3 + (P("rep", "dp", None),) * 6,
        check_vma=False,
    )
```

time: 1620 us -> 742 us (0.46)
  the two profiles are of different devices: /device:TPU:0 before, /device:TPU:19 now
where the time goes in v1:
time: 742 us; the launch traced here: 732 us
  Pallas kernels  481 us (65%)
  matrix products  206 us (28%)
  local copies, waits for them, and re-layouts  33.5 us (5%)
  other arithmetic  11.5 us (2%)
    pallas_call x1, Pallas kernels, tail(): pl.pallas_call(functools.partial(tail_kernel, ny, nz, units), out_shape=o...  481 us
    dot_general x4, matrix products, matmul_t(): lax.dot_general(a, w, (((1,), (1,)), ((), ())), preferred_element_type=F32)  87.9 us
    dot_general x2, matrix products, forward(): up = jnp.dot(a, wu, preferred_element_type=F32)  62.9 us
    dot_general x2, matrix products, forward(): gate = jnp.dot(a, wg, preferred_element_type=F32)  36.1 us
    unnamed x41, local copies, waits for them, and re-layouts  33.5 us
    dot_general x1, matrix products, matmul(): return jnp.dot(a, w, preferred_element_type=F32).astype(BF16)  18.7 us

profile of v1, /device:TPU:19, one launch (start us, length us, event | category | flops | bytes accessed | tf_op | source)
XLA Modules:
  0.0 732.3 jit_solution(17941541097638527052)
XLA Ops:
  0.6 3.1 fusion.8
  3.7 0.0 copy-start.2
  3.7 18.3 %convolution_convert_fusion.1 = bf16[2048,2816]{1,0:T(8,128)(2,1)} fusion(bf16[2,2816,1024]{2,1,0:T(8,128)(2,1)} %refs_12_.1, bf16[1,2048,1024]{2,1,0:T(8,128)(2,1)} %param.12), kind=kOutput, calls=%fused_computation.21 | convolution fusion | flops 11816927232 | bytes 21495808 | tf_op jit(solution)/shard_map/dot_general | solution.py:20
  22.0 0.0 copy-done.2
  22.0 18.2 %fusion.28 = f32[2048,2816]{1,0:T(8,128)} fusion(bf16[2,1024,2816]{2,1,0:T(8,128)(2,1)} %refs_10_.1, bf16[1,2048,1024]{2,1,0:T(8,128)(2,1)S(1)} %copy-done.2, f32[2048]{0:T(1024)S(1)} %add_rsqrt_fusion.1), kind=kOutput, calls=%fused_computation.46 | convolution fusion | flops 11817451520 | bytes 33038336 | tf_op jit(solution)/shard_map/dot_general | solution.py:31
  40.3 28.7 %multiply_convert_fusion.1 = (bf16[2048,2816]{1,0:T(8,128)(2,1)}, f32[2048,2816]{1,0:T(8,128)}) fusion(f32[2048,2816]{1,0:T(8,128)} %fusion.28, bf16[2,1024,2816]{2,1,0:T(8,128)(2,1)} %refs_11_.1, bf16[1,2048,1024]{2,1,0:T(8,128)(2,1)} %param.11, f32[2048]{0:T(1024)S(1)} %add_rsqrt_fusion.1), kind=kOutput, calls=%fused_computation.12 | convolution fusion | flops 11852054528 | bytes 67641344 | tf_op jit(solution)/shard_map/dot_general | solution.py:32
  68.9 0.0 copy-start.3
  68.9 18.7 %fusion.12 = (f32[2048]{0:T(1024)S(1)}, bf16[2048,1024]{1,0:T(8,128)(2,1)S(1)}) fusion(bf16[2048,2816]{1,0:T(8,128)(2,1)} %get-tuple-element.32.refs_3_, bf16[2,2816,1024]{2,1,0:T(8,128)(2,1)} %refs_12_.1, bf16[1,2048,1024]{2,1,0:T(8,128)(2,1)} %param.11), kind=kOutput, calls=%fused_computation.29 | convolution fusion | flops 11821643776 | bytes 25698304 | tf_op jit(solution)/shard_map/dot_general | solution.py:16
  87.6 0.0 copy-start
  87.6 0.0 copy-done.3
  87.6 3.2 fusion.9
  90.8 0.0 copy-done
  90.9 0.0 copy-start.6
  90.9 2.0 copy-done.6
  92.8 17.8 %fusion.17 = f32[2048,2816]{1,0:T(8,128)} fusion(bf16[2048,1024]{1,0:T(8,128)(2,1)S(1)} %get-tuple-element.39.refs_5_, bf16[2,1024,2816]{2,1,0:T(8,128)(2,1)} %refs_10_.1), kind=kOutput, calls=%fused_computation.35 | convolution fusion | flops 11811160064 | bytes 33030144 | tf_op jit(solution)/shard_map/dot_general | solution.py:31
  110.7 34.3 %multiply_convert_fusion = (bf16[2048,2816]{1,0:T(8,128)(2,1)}, bf16[2048,2816]{1,0:T(8,128)(2,1)}, bf16[2048,2816]{1,0:T(8,128)(2,1)}) fusion(f32[2048,2816]{1,0:T(8,128)} %fusion.17, bf16[2048,2816]{1,0:T(8,128)(2,1)} %convolution_convert_fusion.1, bf16[2048,1024]{1,0:T(8,128)(2,1)} %copy-done.6, bf16[2,1024,2816]{2,1,0:T(8,128)(2,1)} %refs_11_.1), kind=kOutput, calls=%fused_computation.10 | convolution fusion | flops 11897667584 | bytes 79167488 | tf_op jit(solution)/shard_map/dot_general | solution.py:32
  144.9 0.0 copy-start.1
  144.9 17.8 %fusion.15 = bf16[2048,1024]{1,0:T(8,128)(2,1)} fusion(bf16[2048,2816]{1,0:T(8,128)(2,1)} %get-tuple-element.28.refs_6_, bf16[2,1024,2816]{2,1,0:T(8,128)(2,1)} %refs_10_.1), kind=kOutput, calls=%fused_computation.33 | convolution fusion | flops 11811160064 | bytes 21495808 | tf_op jit(solution)/shard_map/dot_general | solution.py:20
  162.8 0.0 copy-done.1
  162.8 0.0 copy-start.5
  162.8 19.2 %fusion.14 = (f32[2048]{0:T(1024)S(1)}, bf16[2048,1024]{1,0:T(8,128)(2,1)}) fusion(bf16[2048,1024]{1,0:T(8,128)(2,1)S(1)} %copy-done.1, bf16[2048,1024]{1,0:T(8,128)(2,1)} %fusion.15, bf16[2048,2816]{1,0:T(8,128)(2,1)} %get-tuple-element.29.refs_7_, bf16[2,1024,2816]{2,1,0:T(8,128)(2,1)} %refs_11_.1), kind=kOutput, calls=%fused_computation.31 | convolution fusion | flops 11823740928 | bytes 29892608 | tf_op jit(solution)/shard_map/dot_general | solution.py:20
  181.9 0.0 copy-done.5
  181.9 5.2 fusion.41.refs_4_
  187.2 32.6 %fusion.5 = (bf16[2048,2816]{1,0:T(8,128)(2,1)}, bf16[2048,2816]{1,0:T(8,128)(2,1)}) fusion(f32[2048,2816]{1,0:T(8,128)} %fusion.28, f32[2048,2816]{1,0:T(8,128)} %get-tuple-element.33, bf16[2048,1024]{1,0:T(8,128)(2,1)} %fusion.41.refs_4_, bf16[2,2816,1024]{2,1,0:T(8,128)(2,1)} %refs_12_.1), kind=kOutput, calls=%fused_computation.9 | convolution fusion | flops 11891900416 | bytes 79167488 | tf_op jit(solution)/shard_map/dot_general | solution.py:20
  219.8 480.5 %gradients_and_step.1 = (bf16[2,1024,2816]{2,1,0:T(8,128)(2,1)}, bf16[2,1024,2816]{2,1,0:T(8,128)(2,1)}, bf16[2,2816,1024]{2,1,0:T(8,128)(2,1)}, f32[2,64,2816]{...) custom-call(bf16[2048,1024]{1,0:T(8,128)(2,1)} %get-tuple-element.38, ...), custom_call_target="tpu_custom_call" | custom-call | flops 70866960384 | bytes 209715200 | tf_op jit(solution)/shard_map/gradients_and_step/pallas_call | solution.py:367
  700.3 0.0 copy-start.4
  700.3 0.0 slice-start
  700.3 0.0 slice-start.1
  700.3 11.7 %copy.35 = bf16[2,1024,2816]{2,1,0:T(8,128)(2,1)} copy(bf16[2,1024,2816]{2,1,0:T(8,128)(2,1)} %get-tuple-element.49) | data formatting | bytes 23068672
  712.0 0.0 copy-done.4
  712.0 0.0 slice-start.2
  712.0 5.8 copy.36
  717.8 0.0 slice-done
  717.8 0.7 slice-done.1
  718.5 1.3 slice-done.2
  719.8 5.4 copy.37
  725.2 0.0 copy-done.12
  725.2 1.1 copy.38
  726.3 0.0 copy-done.11
  726.3 1.1 copy.39
  727.4 0.0 copy-done.10
  727.4 1.1 copy.40
  728.5 0.0 copy-done.9
  728.5 1.1 copy.41
  729.6 0.0 copy-done.8
  729.6 1.1 copy.42
  730.7 0.0 copy-done.7
  730.8 1.1 copy.43
  (10 shorter events, 0.0 us)
Async XLA Ops:
  3.7 18.3 %copy-start.2 = (bf16[1,2048,1024]{2,1,0:T(8,128)(2,1)S(1)}, bf16[1,2048,1024]{2,1,0:T(8,128)(2,1)}, u32[]{:S(2)}) copy-start(bf16[1,2048,1024]{2,1,0:T(8,128)(2,1)} %param.11) | copy-start | bytes 12582916
  68.9 18.7 %copy-start.3 = (bf16[1,2048,1024]{2,1,0:T(8,128)(2,1)S(1)}, bf16[1,2048,1024]{2,1,0:T(8,128)(2,1)}, u32[]{:S(2)}) copy-start(bf16[1,2048,1024]{2,1,0:T(8,128)(2,1)} %param.11) | copy-start | bytes 12582916
  87.6 3.3 copy-start
  90.9 2.0 copy-start.6
  144.9 17.8 %copy-start.1 = (bf16[2048,1024]{1,0:T(8,128)(2,1)S(1)}, bf16[2048,1024]{1,0:T(8,128)(2,1)}, u32[]{:S(2)}) copy-start(bf16[2048,1024]{1,0:T(8,128)(2,1)} %copy-done) | copy-start | bytes 12582916
  162.8 19.2 %copy-start.5 = (bf16[1,2048,1024]{2,1,0:T(8,128)(2,1)S(1)}, bf16[1,2048,1024]{2,1,0:T(8,128)(2,1)}, u32[]{:S(2)}) copy-start(bf16[1,2048,1024]{2,1,0:T(8,128)(2,1)} %param.12) | copy-start | bytes 12582916
  700.3 11.7 %copy-start.4 = (bf16[2,1024,2816]{2,1,0:T(8,128)(2,1)S(1)}, bf16[2,1024,2816]{2,1,0:T(8,128)(2,1)}, u32[]{:S(2)}) copy-start(bf16[2,1024,2816]{2,1,0:T(8,128)(2,1)} %get-tuple-element.50) | copy-start | bytes 34603012
  700.3 17.6 %slice-start = ((s8[11534336]{0:T(1024)(128)(4,1)}), s8[4194304]{0:T(1024)(128)(4,1)S(1)}, s32[]{:S(2)}) async-start(s8[11534336]{0:T(1024)(128)(4,1)} %bitcast.58), calls=%async_computation | async-start | bytes 8388608
  700.3 18.2 %slice-start.1 = ((s8[11534336]{0:T(1024)(128)(4,1)}), s8[4194304]{0:T(1024)(128)(4,1)S(1)}, s32[]{:S(2)}) async-start(s8[11534336]{0:T(1024)(128)(4,1)} %bitcast.58), calls=%async_computation.1 | async-start | bytes 8388608
  712.0 7.8 %slice-start.2 = ((s8[11534336]{0:T(1024)(128)(4,1)}), s8[3145728]{0:T(1024)(128)(4,1)S(1)}, s32[]{:S(2)}) async-start(s8[11534336]{0:T(1024)(128)(4,1)} %bitcast.58), calls=%async_computation.2 | async-start | bytes 6291456
  719.8 5.4 copy-start.12
  719.8 6.5 copy-start.11
  719.8 7.6 %copy-start.10 = (f32[2,176,1024]{2,1,0:T(8,128)S(1)}, f32[2,176,1024]{2,1,0:T(8,128)}, u32[]{:S(2)}) copy-start(f32[2,176,1024]{2,1,0:T(8,128)} %get-tuple-element.54) | copy-start | bytes 4325380
  725.2 3.3 copy-start.9
  725.2 4.4 copy-start.8
  725.2 5.5 copy-start.7

commit v2 on v1

--- a/solution.py
+++ b/solution.py
@@ -10,6 +10,7 @@
 F32, BF16 = jnp.float32, jnp.bfloat16
 KINDS = 3
 CHUNK = 256
+ORDER = "cccyccyczyAzfzBfPacfycczyaczfcybczaabfbfaabbb"
 
 
 def matmul(a, w):
@@ -54,20 +55,18 @@
     h1 = x + matmul(act0, wd[0])
     a1, gate1, up1, act1 = forward(h1, wg[1], wu[1])
     dgate1, dup1 = through_product(gate1, up1, matmul_t(dy, wd[1]))
-    da = matmul_t(dgate1, wg[1]) + matmul_t(dup1, wu[1])
-    dh0 = dy + through_norm(h1, da)
-    dgate0, dup0 = through_product(gate0, up0, matmul_t(dh0, wd[0]))
-    return (a0, dgate0, dup0, act0, dh0), (a1, dgate1, dup1, act1, dy)
+    return (a0, act0), (a1, dgate1, dup1, act1, dy), (h1, gate0, up0)
 
 
 def tail_kernel(ny, nz, units, *refs):
-    layers = 2
-    acts = [refs[5 * n : 5 * n + 5] for n in range(layers)]
-    refs = refs[5 * layers :]
+    a0, act0, a1, dgate1, dup1, act1, dy, h1, gate0, up0, wg_view, wu_view, dgate1_view, dup1_view = refs[:14]
+    refs = refs[14:]
     ws, ms, vs, nws, nms, nvs = (refs[3 * i : 3 * i + 3] for i in range(6))
     zrecv = refs[18:20]
-    (g0, g1, c0, c1, y0, y1, cs0, cs1, mst0, mst1, vst0, vst1, wst0, wst1, zst0, zst1, at, ach, bt,
-     c_s, c_r, y_s, y_r, z_s, z_r, agz_s, agz_r, agy_s, agy_r, agc_s, agc_r, asem, bsem, lsem, osem) = refs[20:]
+    dgate0, dup0, dh0 = refs[20:23]
+    acts = ((a0, dgate0, dup0, act0, dh0), (a1, dgate1, dup1, act1, dy))
+    (g0, g1, c0, c1, y0, y1, cs0, cs1, mst0, mst1, vst0, vst1, wst0, wst1, zst0, zst1, at, gu, bt,
+     c_s, c_r, y_s, y_r, z_s, z_r, agz_s, agz_r, agy_s, agy_r, agc_s, agc_r, asem, bsem, lsem, osem, psem) = refs[23:]
     G, C, Y, CS = (g0, g1), (c0, c1), (y0, y1), (cs0, cs1)
     MST, VST, WST, ZST = (mst0, mst1), (vst0, vst1), (wst0, wst1), (zst0, zst1)
 
@@ -136,12 +135,8 @@
         yy = y if h else 1 - y
         steps, tiles = tokens // CHUNK, cols // CHUNK
 
-        def get_a(s):
-            where = pl.ds(pl.multiple_of(s * CHUNK, CHUNK), CHUNK)
-            return pltpu.make_async_copy(lhs.at[where, pl.ds(pl.multiple_of(yy * half, 128), half)], at.at[where, :half], asem.at[0])
-
         def get_b(n, slot):
-            return pltpu.make_async_copy(rhs.at[:, pl.ds(pl.multiple_of(n * CHUNK, CHUNK), CHUNK)], bt.at[slot], bsem.at[slot])
+            return pltpu.make_async_copy(rhs.at[:, pl.ds(pl.multiple_of(n * CHUNK, CHUNK), CHUNK)], bt.at[slot], bsem.at[slot, 0])
 
         whole = pltpu.make_async_copy(lhs.at[:, pl.ds(pl.multiple_of(yy * half, 128), half)], at.at[:, :half], asem.at[0])
         whole.start()
@@ -170,6 +165,151 @@
 
         c_copy(u, h).start()
         last_c[t] = (u, h)
+
+    tokens, dim = h1.shape
+    tile = 2 * G[0].shape[3]
+    block = nz * G[0].shape[3]
+    spare = len([1 for layer, kind in units if kind != 2]) // 2
+
+    def across(view, w_view, after):
+        matrix = pltpu.make_async_copy(w_view.at[1], G[0].at[pl.ds(spare, 2)], psem.at[0])
+        matrix.start()
+
+        def get(s, slot):
+            return pltpu.make_async_copy(view.at[pl.ds(s * 2, 2)], CS[0].at[pl.ds(slot * 2, 2)], asem.at[slot])
+
+        if last_c[0] is not None:
+            c_copy(*last_c[0]).wait_send()
+            last_c[0] = None
+        get(0, 0).start()
+        if after is not None:
+            after.get(0, 0)
+        matrix.wait()
+
+        @pl.loop(0, tokens // tile)
+        def _(s):
+            slot = lax.rem(s, 2)
+            rows = pl.ds(pl.multiple_of(s * tile, tile), tile)
+
+            @pl.when(s + 1 < tokens // tile)
+            def _():
+                get(s + 1, 1 - slot).start()
+                if after is not None:
+                    after.get(s + 1, 1 - slot)
+
+            get(s, slot).wait()
+            lhs = CS[0][pl.ds(slot * 2, 2)].reshape(tile, -1)
+            for q in range(4):
+                rhs = G[0][spare + q // 2, q % 2].reshape(block, -1)
+                part = matmul_t(lhs, rhs)
+                cols = slice(q * block, (q + 1) * block)
+                if after is None:
+                    at[rows, cols] = part
+                else:
+                    at[rows, cols] = at[rows, cols] + part
+            if after is not None:
+                after.use(s, slot, rows)
+
+    class Norm:
+        @staticmethod
+        def copies(s, slot):
+            rows = pl.ds(pl.multiple_of(s * tile, tile), tile)
+            return [
+                pltpu.make_async_copy(src.at[rows, :], G[1].at[1, slot, k, pl.ds(0, tile), :], psem.at[1 + 2 * slot + k])
+                for k, src in enumerate((h1, dy))
+            ]
+
+        @staticmethod
+        def get(s, slot):
+            for copy in Norm.copies(s, slot):
+                copy.start()
+
+        @staticmethod
+        def use(s, slot, rows):
+            for copy in Norm.copies(s, slot):
+                copy.wait()
+            h, by = (G[1][1, slot, k, :tile, :] for k in range(2))
+            at[rows, :dim] = by + through_norm(h, at[rows, :dim])
+
+    def dh0_out():
+        return pltpu.make_async_copy(at.at[:, :dim], dh0, psem.at[0])
+
+    def into_product():
+        part = tokens // 4
+        ff = gate0.shape[1]
+        piece = CHUNK // 2
+
+        def get_w(n, slot):
+            return [
+                pltpu.make_async_copy(
+                    ws[2].at[0, pl.ds(pl.multiple_of(n * CHUNK + k * piece, piece), piece), :],
+                    G[1].at[1, slot, k, pl.ds(0, piece), :],
+                    psem.at[1 + 2 * slot + k],
+                )
+                for k in range(2)
+            ]
+
+        def where(n, m):
+            return pl.ds(m * part, part), pl.ds(pl.multiple_of(n * CHUNK, CHUNK), CHUNK)
+
+        def get_gu(n, m):
+            return [pltpu.make_async_copy(src.at[*where(n, m)], gu.at[m % 2, k], bsem.at[m % 2, k]) for k, src in enumerate((gate0, up0))]
+
+        def put(n, m):
+            return [
+                pltpu.make_async_copy(bt.at[m % 2, pl.ds(k * part, part), :], dst.at[*where(n, m)], asem.at[2 + 2 * (m % 2) + k])
+                for k, dst in enumerate((dgate0, dup0))
+            ]
+
+        def each(copies, act):
+            for copy in copies:
+                act(copy)
+
+        def begin(copy):
+            copy.start()
+
+        def end(copy):
+            copy.wait()
+
+        each(get_w(0, 0), begin)
+        each(get_gu(0, 0), begin)
+
+        @pl.loop(0, ff // CHUNK)
+        def _(n):
+            slot = lax.rem(n, 2)
+
+            @pl.when(n + 1 < ff // CHUNK)
+            def _():
+                each(get_w(n + 1, 1 - slot), begin)
+
+            each(get_w(n, slot), end)
+            w = jnp.concatenate([G[1][1, slot, k, :piece, :] for k in range(2)], axis=0)
+            for m in range(4):
+                if m < 3:
+                    each(get_gu(n, m + 1), begin)
+                else:
+
+                    @pl.when(n + 1 < ff // CHUNK)
+                    def _():
+                        each(get_gu(n + 1, 0), begin)
+
+                dact = matmul_t(at[m * part : (m + 1) * part, :dim], w)
+                each(get_gu(n, m), end)
+                if m >= 2:
+                    each(put(n, m - 2), end)
+                else:
+
+                    @pl.when(n > 0)
+                    def _():
+                        each(put(n - 1, m + 2), end)
+
+                dgate, dup = through_product(gu[m % 2, 0], gu[m % 2, 1], dact)
+                bt[m % 2, :part, :] = dgate
+                bt[m % 2, part : 2 * part, :] = dup
+                each(put(n, m), begin)
+
+        for m in (2, 3):
+            each(put(ff // CHUNK - 1, m), end)
 
     def pieces(t, body):
         rows, cols = rows_of(t)
@@ -294,18 +434,21 @@
             stages[s](done[s])
             done[s] += 1
 
-    for u in range(n):
-        compute(u, 0)
-        if u:
-            run("y")
-        compute(u, 1)
-        if u == 2:
-            run("z")
-        if u == 3:
-            run("z")
-        if u == 4:
-            run("fz")
-    run("y" + "fza" + "fzab" + "fzab" + "fab" + "fab" + "ab" + "b")
+    halves = 0
+    for step in ORDER:
+        if step == "c":
+            compute(*divmod(halves, 2))
+            halves += 1
+        elif step == "A":
+            across(dgate1_view, wg_view, None)
+        elif step == "B":
+            across(dup1_view, wu_view, Norm)
+            dh0_out().start()
+        elif step == "P":
+            into_product()
+            dh0_out().wait()
+        else:
+            run(step)
     assert all(v == n for v in done.values()), done
 
     for u in range(n):
@@ -330,11 +473,11 @@
         own_out(pending[t]).wait()
 
 
-def tail(ny, nz, acts, ws, ms, vs):
+def tail(ny, nz, acts0, acts1, rest, ws, ms, vs):
     units = ((1, 0), (1, 1), (1, 2), (0, 0), (0, 1), (0, 2))
     rg, ff = ms[0].shape[1:]
     rd, dim = ms[2].shape[1:]
-    tokens = acts[0][0].shape[0]
+    tokens = acts1[0].shape[0]
     shapes = ((rg, ff), (rd, dim))
     slots = (4, 2)
     n = len(units)
@@ -343,6 +486,7 @@
         [jax.ShapeDtypeStruct(w.shape, BF16) for w in ws]
         + [jax.ShapeDtypeStruct(m.shape, F32) for m in (*ms, *vs)]
         + [jax.ShapeDtypeStruct((s, nz - 1, *shape), BF16) for s, shape in zip(slots, shapes)]
+        + [jax.ShapeDtypeStruct(s, BF16) for s in ((tokens, ff), (tokens, ff), (tokens, dim))]
     )
     scratch = (
         [pltpu.VMEM((s, 2, nz, *shape), BF16) for s, shape in zip(slots, shapes)]
@@ -356,24 +500,33 @@
     half = nz * 2 * max(rg, rd)
     scratch += [
         pltpu.VMEM((tokens, half), BF16),
-        pltpu.VMEM((2, 16, half), BF16),
+        pltpu.VMEM((2, 2, tokens // 4, CHUNK), F32),
         pltpu.VMEM((2, tokens, CHUNK), BF16),
     ]
     dma = pltpu.SemaphoreType.DMA
     for count in (2, nz, nz - 1, nz - 1, nz, 2 * nz):
         scratch += [dma((n, count)), dma((n, count))]
-    scratch += [dma((2,)), dma((2,)), dma((2, 4)), dma((2, 3))]
-    flops = 2 * n * tokens * ff * dim
+    scratch += [dma((6,)), dma((2, 2)), dma((2, 4)), dma((2, 3)), dma((5,))]
+    flops = 3 * n * tokens * ff * dim
     res = pl.pallas_call(
         functools.partial(tail_kernel, ny, nz, units),
         out_shape=outs,
-        in_specs=[any_spec] * (10 + 9),
+        in_specs=[any_spec] * (14 + 9),
         out_specs=[any_spec] * len(outs),
         scratch_shapes=scratch,
         compiler_params=pltpu.CompilerParams(collective_id=0, has_side_effects=True, vmem_limit_bytes=67043328),
         cost_estimate=pl.CostEstimate(flops=flops, bytes_accessed=200 << 20, transcendentals=0),
         name="gradients_and_step",
-    )(*acts[0], *acts[1], *ws, *ms, *vs)
+    )(
+        *acts0,
+        *acts1,
+        *rest,
+        *(w.reshape(-1, 2, 2, nz, rg, ff) for w in ws[:2]),
+        *(t.reshape(-1, rg, ff) for t in acts1[1:3]),
+        *ws,
+        *ms,
+        *vs,
+    )
     return tuple(res[:9])
 
 
@@ -384,7 +537,7 @@
     def step(x, dy, *arrays):
         ws, ms, vs = (arrays[i : i + 3] for i in (0, 3, 6))
         acts = chain(x[0], dy[0], *ws)
-        return tail(ny, nz, acts, ws, ms, vs)
+        return tail(ny, nz, *acts, ws, ms, vs)
 
     mom = P(None, "dp", None)
     return jax.shard_map(

time: 742 us -> 678 us (0.914)
  the two profiles are of different devices: /device:TPU:19 before, /device:TPU:0 now
where the time goes in v2:
time: 678 us; the launch traced here: 667 us
  Pallas kernels  491 us (72%)
  matrix products  135 us (20%)
  local copies, waits for them, and re-layouts  33.5 us (5%)
    pallas_call x1, Pallas kernels, tail(): pl.pallas_call(functools.partial(tail_kernel, ny, nz, units), out_shape=o...  491 us
    dot_general x2, matrix products, forward(): up = jnp.dot(a, wu, preferred_element_type=F32)  63.1 us
    dot_general x2, matrix products, forward(): gate = jnp.dot(a, wg, preferred_element_type=F32)  36 us
    unnamed x37, local copies, waits for them, and re-layouts  33.5 us
    dot_general x1, matrix products, matmul_t(): lax.dot_general(a, w, (((1,), (1,)), ((), ())), preferred_element_type=F32)  18.3 us
    dot_general x1, matrix products, matmul(): return jnp.dot(a, w, preferred_element_type=F32).astype(BF16)  17.9 us

profile of v2, /device:TPU:0, one launch (start us, length us, event | category | flops | bytes accessed | tf_op | source)
XLA Modules:
  0.0 667.1 jit_solution(11437567506510124441)
XLA Ops:
  0.6 3.1 fusion.4
  3.7 0.0 copy-start
  3.7 18.3 %convolution_convert_fusion = bf16[2048,2816]{1,0:T(8,128)(2,1)} fusion(bf16[2,2816,1024]{2,1,0:T(8,128)(2,1)} %refs_16_.1, bf16[1,2048,1024]{2,1,0:T(8,128)(2,1)} %param.12), kind=kOutput, calls=%fused_computation.9 | convolution fusion | flops 11816927232 | bytes 21495808 | tf_op jit(solution)/shard_map/dot_general | solution.py:21
  22.0 0.0 copy-done
  22.0 18.3 %fusion.17.refs_8_ = f32[2048,2816]{1,0:T(8,128)} fusion(bf16[2,1024,2816]{2,1,0:T(8,128)(2,1)} %refs_14_.1, bf16[1,2048,1024]{2,1,0:T(8,128)(2,1)S(1)} %copy-done, f32[2048]{0:T(1024)S(1)} %add_rsqrt_fusion.1), kind=kOutput, calls=%fused_computation.28 | convolution fusion | flops 11817451520 | bytes 33038336 | tf_op jit(solution)/shard_map/dot_general | solution.py:32
  40.3 28.6 %multiply_convert_fusion.1 = (bf16[2048,2816]{1,0:T(8,128)(2,1)}, f32[2048,2816]{1,0:T(8,128)}) fusion(f32[2048,2816]{1,0:T(8,128)} %fusion.17.refs_8_, bf16[2,1024,2816]{2,1,0:T(8,128)(2,1)} %refs_15_.1, bf16[1,2048,1024]{2,1,0:T(8,128)(2,1)} %param.11, f32[2048]{0:T(1024)S(1)} %add_rsqrt_fusion.1), kind=kOutput, calls=%fused_computation.7 | convolution fusion | flops 11852054528 | bytes 67641344 | tf_op jit(solution)/shard_map/dot_general | solution.py:33
  68.9 0.0 copy-start.1
  68.9 17.9 %fusion.6 = (f32[2048]{0:T(1024)S(1)}, bf16[2048,1024]{1,0:T(8,128)(2,1)S(1)}) fusion(bf16[2048,2816]{1,0:T(8,128)(2,1)} %get-tuple-element.30.refs_1_, bf16[2,2816,1024]{2,1,0:T(8,128)(2,1)} %refs_16_.1, bf16[1,2048,1024]{2,1,0:T(8,128)(2,1)} %param.11), kind=kOutput, calls=%fused_computation.16 | convolution fusion | flops 11821643776 | bytes 25698304 | tf_op jit(solution)/shard_map/dot_general | solution.py:17
  86.9 0.0 copy-start.3
  86.9 0.0 copy-done.1
  86.9 3.2 fusion.5
  90.1 0.0 copy-done.3
  90.1 0.0 copy-start.4
  90.1 2.0 copy-done.4
  92.1 17.8 %fusion.8 = f32[2048,2816]{1,0:T(8,128)} fusion(bf16[2048,1024]{1,0:T(8,128)(2,1)S(1)} %get-tuple-element.35.refs_2_, bf16[2,1024,2816]{2,1,0:T(8,128)(2,1)} %refs_14_.1), kind=kOutput, calls=%fused_computation.19 | convolution fusion | flops 11811160064 | bytes 33030144 | tf_op jit(solution)/shard_map/dot_general | solution.py:32
  109.8 34.4 %multiply_convert_fusion = (bf16[2048,2816]{1,0:T(8,128)(2,1)}, bf16[2048,2816]{1,0:T(8,128)(2,1)}, bf16[2048,2816]{1,0:T(8,128)(2,1)}) fusion(f32[2048,2816]{1,0:T(8,128)} %fusion.8, bf16[2048,2816]{1,0:T(8,128)(2,1)} %convolution_convert_fusion, bf16[2048,1024]{1,0:T(8,128)(2,1)} %copy-done.4, bf16[2,1024,2816]{2,1,0:T(8,128)(2,1)} %refs_15_.1), kind=kOutput, calls=%fused_computation.5 | convolution fusion | flops 11897667584 | bytes 79167488 | tf_op jit(solution)/shard_map/dot_general | solution.py:33
  144.3 490.8 %gradients_and_step.1 = (bf16[2,1024,2816]{2,1,0:T(8,128)(2,1)}, bf16[2,1024,2816]{2,1,0:T(8,128)(2,1)}, bf16[2,2816,1024]{2,1,0:T(8,128)(2,1)}, f32[2,64,2816]{...) custom-call(bf16[2048,1024]{1,0:T(8,128)(2,1)} %get-tuple-element.34, ...), custom_call_target="tpu_custom_call" | custom-call | flops 106300440576 | bytes 209715200 | tf_op jit(solution)/shard_map/gradients_and_step/pallas_call | solution.py:511
  635.1 0.0 copy-start.2
  635.2 0.0 slice-start
  635.2 0.0 slice-start.1
  635.2 11.7 %copy.31 = bf16[2,1024,2816]{2,1,0:T(8,128)(2,1)} copy(bf16[2,1024,2816]{2,1,0:T(8,128)(2,1)} %get-tuple-element.45) | data formatting | bytes 23068672
  646.8 0.0 copy-done.2
  646.9 0.0 slice-start.2
  646.9 5.8 copy.32
  652.7 0.0 slice-done
  652.7 0.7 slice-done.1
  653.4 1.3 slice-done.2
  654.7 0.0 copy-start.10
  654.7 0.0 copy-start.9
  654.7 0.0 copy-start.8
  654.7 5.4 copy.33
  660.1 0.0 copy-done.10
  660.1 0.0 copy-start.7
  660.1 0.0 copy-start.6
  660.1 0.0 copy-start.5
  660.1 1.1 copy.34
  661.2 0.0 copy-done.9
  661.2 1.1 copy.35
  662.3 0.0 copy-done.8
  662.3 1.1 copy.36
  663.4 0.0 copy-done.7
  663.4 1.1 copy.37
  664.5 0.0 copy-done.6
  664.5 1.1 copy.38
  665.6 0.0 copy-done.5
  665.6 1.1 copy.39
  (3 shorter events, 0.0 us)
Async XLA Ops:
  3.7 18.3 %copy-start = (bf16[1,2048,1024]{2,1,0:T(8,128)(2,1)S(1)}, bf16[1,2048,1024]{2,1,0:T(8,128)(2,1)}, u32[]{:S(2)}) copy-start(bf16[1,2048,1024]{2,1,0:T(8,128)(2,1)} %param.11) | copy-start | bytes 12582916
  68.9 18.0 %copy-start.1 = (bf16[1,2048,1024]{2,1,0:T(8,128)(2,1)S(1)}, bf16[1,2048,1024]{2,1,0:T(8,128)(2,1)}, u32[]{:S(2)}) copy-start(bf16[1,2048,1024]{2,1,0:T(8,128)(2,1)} %param.11) | copy-start | bytes 12582916
  86.9 3.2 copy-start.3
  90.1 2.0 copy-start.4
  635.1 11.7 %copy-start.2 = (bf16[2,1024,2816]{2,1,0:T(8,128)(2,1)S(1)}, bf16[2,1024,2816]{2,1,0:T(8,128)(2,1)}, u32[]{:S(2)}) copy-start(bf16[2,1024,2816]{2,1,0:T(8,128)(2,1)} %get-tuple-element.46) | copy-start | bytes 34603012
  635.2 17.6 %slice-start = ((s8[11534336]{0:T(1024)(128)(4,1)}), s8[4194304]{0:T(1024)(128)(4,1)S(1)}, s32[]{:S(2)}) async-start(s8[11534336]{0:T(1024)(128)(4,1)} %bitcast.46), calls=%async_computation | async-start | bytes 8388608
  635.2 18.2 %slice-start.1 = ((s8[11534336]{0:T(1024)(128)(4,1)}), s8[4194304]{0:T(1024)(128)(4,1)S(1)}, s32[]{:S(2)}) async-start(s8[11534336]{0:T(1024)(128)(4,1)} %bitcast.46), calls=%async_computation.1 | async-start | bytes 8388608
  646.9 7.8 %slice-start.2 = ((s8[11534336]{0:T(1024)(128)(4,1)}), s8[3145728]{0:T(1024)(128)(4,1)S(1)}, s32[]{:S(2)}) async-start(s8[11534336]{0:T(1024)(128)(4,1)} %bitcast.46), calls=%async_computation.2 | async-start | bytes 6291456
  654.7 5.4 copy-start.10
  654.7 6.5 copy-start.9
  654.7 7.6 %copy-start.8 = (f32[2,176,1024]{2,1,0:T(8,128)S(1)}, f32[2,176,1024]{2,1,0:T(8,128)}, u32[]{:S(2)}) copy-start(f32[2,176,1024]{2,1,0:T(8,128)} %get-tuple-element.50) | copy-start | bytes 4325380
  660.1 3.3 copy-start.7
  660.1 4.4 copy-start.6
  660.1 5.5 copy-start.5
